TPU v7x, 32 devices: a 4x4x1 block of a 4x4x8 slice. The times are simulated.
32 devices in a mesh: dp: 1 (over z), tp: 4 (over y), ep: 8 (over x, core).
Axes of the slice: x: 4, y: 4, z: 1, core: 2. Of those that a mesh axis runs over, the one named last changes fastest.
The devices are a block of a 4x4x8 slice.
Arguments:
- hidden: bfloat16 [2048, 768], P(('dp', 'ep'))
- write_pos: int32 [2048], P(('dp', 'ep'))
- enc_mask: int32 [2048, 32], P(('dp', 'ep'))
- expert_idx: int32 [2048], P(('dp', 'ep'))
- self_keys: bfloat16 [2, 2048, 12, 32, 64], P(None, ('dp', 'ep'), 'tp')
- self_values: bfloat16 [2, 2048, 12, 32, 64], P(None, ('dp', 'ep'), 'tp')
- cross_keys: bfloat16 [2, 2048, 12, 32, 64], P(None, ('dp', 'ep'), 'tp')
- cross_values: bfloat16 [2, 2048, 12, 32, 64], P(None, ('dp', 'ep'), 'tp')
- rel_bias: float32 [12, 32], P('tp')
- norm_scale: float32 [2, 3, 768], replicated
- w_query: bfloat16 [2, 768, 768], P(None, None, 'tp')
- w_key: bfloat16 [2, 768, 768], P(None, None, 'tp')
- w_value: bfloat16 [2, 768, 768], P(None, None, 'tp')
- w_out: bfloat16 [2, 768, 768], P(None, 'tp')
- w_cross_query: bfloat16 [2, 768, 768], P(None, None, 'tp')
- w_cross_out: bfloat16 [2, 768, 768], P(None, 'tp')
- dense_gate: bfloat16 [768, 3072], P(None, 'tp')
- dense_up: bfloat16 [768, 3072], P(None, 'tp')
- dense_down: bfloat16 [3072, 768], P('tp')
- router: float32 [768, 16], replicated
- exp_gate: bfloat16 [16, 768, 3072], P('ep', None, 'tp')
- exp_up: bfloat16 [16, 768, 3072], P('ep', None, 'tp')
- exp_down: bfloat16 [16, 3072, 768], P('ep', 'tp')
Outputs:
- output 1: bfloat16 [2048, 768], P(('dp', 'ep'))
- output 2: bfloat16 [2, 2048, 12, 32, 64], P(None, ('dp', 'ep'), 'tp')
- output 3: bfloat16 [2, 2048, 12, 32, 64], P(None, ('dp', 'ep'), 'tp')
All inputs are finite; a program needn't handle non-finite values.
Results may differ from a plain program's by a relative error of at most 0.02.
Values are sent between devices in bfloat16 or wider.
A program may use at most 768 MiB of HBM per device.

v0:
```python
import jax
import jax.numpy as jnp
from jax import lax
from jax.sharding import PartitionSpec as P

EPS = 1e-6
NEG_BIG = -1e9


def rms_norm(h_cur, scale):
    h_float = h_cur.astype(jnp.float32)
    inv_rms = lax.rsqrt(jnp.mean(h_float * h_float, axis=-1, keepdims=True) + EPS)
    return (h_float * inv_rms * scale).astype(jnp.bfloat16)


def add_residual(h_cur, delta):
    return (h_cur.astype(jnp.float32) + delta.astype(jnp.float32)).astype(jnp.bfloat16)


def project(normed, weight):
    return jnp.dot(normed, weight, preferred_element_type=jnp.float32)


def self_attention(normed, write_pos, keys, values, w_query, w_key, w_value, w_out, rel_bias):
    tokens = normed.shape[0]
    heads, cache_len = rel_bias.shape
    head_dim = keys.shape[-1]
    query = project(normed, w_query).astype(jnp.bfloat16).reshape(tokens, heads, head_dim)
    key_new = project(normed, w_key).astype(jnp.bfloat16).reshape(tokens, heads, head_dim)
    value_new = project(normed, w_value).astype(jnp.bfloat16).reshape(tokens, heads, head_dim)
    distance = write_pos[:, None] - jnp.arange(cache_len)[None, :]
    at_slot = (distance == 0)[:, None, :, None]
    keys = jnp.where(at_slot, key_new[:, :, None, :], keys)
    values = jnp.where(at_slot, value_new[:, :, None, :], values)
    scores = jnp.einsum('thd,thld->thl', query, keys, preferred_element_type=jnp.float32)
    bias = jnp.take(rel_bias, jnp.maximum(distance, 0), axis=1)
    scores = jnp.where((distance >= 0)[:, None, :], scores + jnp.swapaxes(bias, 0, 1), NEG_BIG)
    attn_prob = jax.nn.softmax(scores, axis=-1).astype(jnp.bfloat16)
    context = jnp.einsum('thl,thld->thd', attn_prob, values, preferred_element_type=jnp.float32).astype(jnp.bfloat16)
    return project(context.reshape(tokens, heads * head_dim), w_out), keys, values


def cross_attention(normed, enc_mask, keys, values, w_query, w_out):
    tokens = normed.shape[0]
    heads = keys.shape[1]
    head_dim = keys.shape[-1]
    query = project(normed, w_query).astype(jnp.bfloat16).reshape(tokens, heads, head_dim)
    scores = jnp.einsum('thd,thsd->ths', query, keys, preferred_element_type=jnp.float32)
    scores = jnp.where((enc_mask > 0)[:, None, :], scores, NEG_BIG)
    attn_prob = jax.nn.softmax(scores, axis=-1).astype(jnp.bfloat16)
    context = jnp.einsum('ths,thsd->thd', attn_prob, values, preferred_element_type=jnp.float32).astype(jnp.bfloat16)
    return project(context.reshape(tokens, heads * head_dim), w_out)


def gated_ffn(normed, w_gate, w_up, w_down):
    product = (jax.nn.gelu(project(normed, w_gate)) * project(normed, w_up)).astype(jnp.bfloat16)
    return project(product, w_down)


def switch_layer(normed, expert_idx, router, exp_gate, exp_up, exp_down):
    tokens = normed.shape[0]
    experts = router.shape[1]
    capacity = (2 * tokens + experts - 1) // experts
    logits = jnp.dot(normed.astype(jnp.float32), router, preferred_element_type=jnp.float32)
    route_prob = jax.nn.softmax(logits, axis=-1)
    onehot = (expert_idx[:, None] == jnp.arange(experts)[None, :]).astype(jnp.int32)
    gate = jnp.sum(route_prob * onehot, axis=-1)
    slot = jnp.sum((jnp.cumsum(onehot, axis=0) - onehot) * onehot, axis=-1)
    dispatch = (onehot[:, :, None] * (slot[:, None, None] == jnp.arange(capacity)[None, None, :])).astype(jnp.bfloat16)
    buffers = jnp.einsum('tec,td->ecd', dispatch, normed, preferred_element_type=jnp.float32).astype(jnp.bfloat16)
    received = lax.all_to_all(buffers, 'ep', 0, 1, tiled=True)
    gate_in = jnp.einsum('ecd,edf->ecf', received, exp_gate, preferred_element_type=jnp.float32)
    lin_in = jnp.einsum('ecd,edf->ecf', received, exp_up, preferred_element_type=jnp.float32)
    product = (jax.nn.gelu(gate_in) * lin_in).astype(jnp.bfloat16)
    expert_out = jnp.einsum('ecf,efd->ecd', product, exp_down, preferred_element_type=jnp.float32).astype(jnp.bfloat16)
    expert_out = lax.psum(expert_out, 'tp')
    returned = lax.all_to_all(expert_out, 'ep', 1, 0, tiled=True)
    combined = jnp.einsum('tec,ecd->td', dispatch, returned, preferred_element_type=jnp.float32)
    return gate[:, None] * combined


def decode_body(hidden, write_pos, enc_mask, expert_idx, self_keys, self_values, cross_keys, cross_values, rel_bias, norm_scale, w_query, w_key, w_value, w_out, w_cross_query, w_cross_out, dense_gate, dense_up, dense_down, router, exp_gate, exp_up, exp_down):
    h_cur = hidden
    keys_list = []
    values_list = []
    for layer in range(2):
        normed = rms_norm(h_cur, norm_scale[layer, 0])
        attn_part, keys_new, values_new = self_attention(normed, write_pos, self_keys[layer], self_values[layer], w_query[layer], w_key[layer], w_value[layer], w_out[layer], rel_bias)
        h_cur = add_residual(h_cur, lax.psum(attn_part.astype(jnp.bfloat16), 'tp'))
        keys_list.append(keys_new)
        values_list.append(values_new)
        normed = rms_norm(h_cur, norm_scale[layer, 1])
        cross_part = cross_attention(normed, enc_mask, cross_keys[layer], cross_values[layer], w_cross_query[layer], w_cross_out[layer])
        h_cur = add_residual(h_cur, lax.psum(cross_part.astype(jnp.bfloat16), 'tp'))
        normed = rms_norm(h_cur, norm_scale[layer, 2])
        if layer == 0:
            ffn_part = gated_ffn(normed, dense_gate, dense_up, dense_down)
            h_cur = add_residual(h_cur, lax.psum(ffn_part.astype(jnp.bfloat16), 'tp'))
        else:
            h_cur = add_residual(h_cur, switch_layer(normed, expert_idx, router, exp_gate, exp_up, exp_down))
    return h_cur, jnp.stack(keys_list), jnp.stack(values_list)


def solution(mesh):
    batch = ('dp', 'ep')
    row_spec = P(batch, None)
    vec_spec = P(batch)
    cache_spec = P(None, batch, 'tp', None, None)
    col_spec = P(None, None, 'tp')
    out_rows = P(None, 'tp', None)
    in_specs = (row_spec, vec_spec, row_spec, vec_spec, cache_spec, cache_spec, cache_spec, cache_spec, P('tp', None), P(), col_spec, col_spec, col_spec, out_rows, col_spec, out_rows, P(None, 'tp'), P(None, 'tp'), P('tp', None), P(), P('ep', None, 'tp'), P('ep', None, 'tp'), P('ep', 'tp', None))
    out_specs = (row_spec, cache_spec, cache_spec)
    return jax.shard_map(decode_body, mesh=mesh, in_specs=in_specs, out_specs=out_specs, check_vma=False)
```

profile of v0, /device:TPU:97, one launch (start us, length us, event | category | flops | bytes accessed | tf_op | source)
XLA Modules:
  0.0 445.5 jit_solution(15016434307098550108)
XLA Ops:
  7.3 0.9 fusion.126
  8.8 1.2 fusion.43
  10.0 0.8 copy.44
  10.7 1.4 slice_reduce_fusion.1
  12.6 1.4 convolution_convert_fusion.13
  14.1 1.5 convolution_convert_fusion.12
  15.6 1.5 convolution_convert_fusion.14
  17.1 3.2 multiply_reduce_fusion.7
  20.4 4.4 copy.56
  24.8 28.0 %gather_fusion = f32[8192,3]{1,0:T(8,128)} fusion(f32[3,32]{0,1:T(8,128)S(1)} %copy.44, s32[8192]{0:T(1024)S(1)} %broadcast_clamp_fusion), kind=kCustom, calls=%fused_computation.clone | custom fusion | bytes 229376 | tf_op jit(solution)/shard_map/jit(_take)/gather | solution.py:36
  52.8 7.9 %fusion.22 = f32[256,3,32]{1,2,0:T(8,128)} fusion(f32[256,3,32]{1,2,0:T(8,128)} %copy.56, f32[256,32,3]{2,1,0:T(8,128)} %bitcast.182, pred[256,32]{1,0:T(8,128)(4,1)S(1)} %copy.42, pred[256,32]{1,0:T(8,128)(4,1)S(1)} %copy.41), kind=kOutput, calls=%fused_computation.50 | output fusion | flops 173630 | bytes 311296 | tf_op jit(solution)/shard_map/div | solution.py:38
  60.6 3.7 copy.99
  64.3 2.9 multiply_reduce_fusion.6
  67.3 1.0 convolution_convert_fusion.6
  68.6 0.8 broadcast_compare_fusion.1
  69.5 38.0 %all-reduce.7.cloned.1.call-done = bf16[256,768]{1,0:T(8,128)(2,1)} async-done(((bf16[256,768]{1,0:T(8,128)(2,1)}), bf16[256,768]{1,0:T(8,128)(2,1)}) %all-reduce.7.cloned.1.call-update) | async-done | bytes 393232 | tf_op jit(solution)/shard_map/psum | solution.py:89
  107.5 1.2 fusion.47
  108.7 1.5 convolution_convert_fusion.11
  110.2 2.9 multiply_reduce_fusion.5
  113.1 4.4 copy.68
  117.6 8.1 %fusion.23 = f32[256,3,32]{1,2,0:T(8,128)} fusion(f32[256,3,32]{1,2,0:T(8,128)} %copy.68, pred[256,32]{1,0:T(8,128)(4,1)S(1)} %copy.45), kind=kOutput, calls=%fused_computation.51 | output fusion | flops 149054 | bytes 204800 | tf_op jit(solution)/shard_map/div | solution.py:50
  125.7 3.6 copy.101
  129.3 2.7 multiply_reduce_fusion.4
  132.0 2.0 convolution_convert_fusion.5
  134.2 37.6 %all-reduce.9.cloned.1.call-done = bf16[256,768]{1,0:T(8,128)(2,1)} async-done(((bf16[256,768]{1,0:T(8,128)(2,1)}), bf16[256,768]{1,0:T(8,128)(2,1)}) %all-reduce.9.cloned.1.call-update) | async-done | bytes 393232 | tf_op jit(solution)/shard_map/psum | solution.py:94
  171.8 1.3 fusion.51
  173.1 2.7 fusion.119
  175.7 3.6 convolution_convert_fusion.4
  179.7 37.5 %all-reduce.11.cloned.1.call-done = bf16[256,768]{1,0:T(8,128)(2,1)} async-done(((bf16[256,768]{1,0:T(8,128)(2,1)}), bf16[256,768]{1,0:T(8,128)(2,1)}) %all-reduce.11.cloned.1.call-update) | async-done | bytes 393232 | tf_op jit(solution)/shard_map/psum | solution.py:98
  217.1 1.2 fusion.63
  218.4 1.3 convolution_convert_fusion.9
  219.7 1.3 convolution_convert_fusion.8
  221.0 1.3 convolution_convert_fusion.10
  222.4 3.2 multiply_reduce_fusion.3
  225.7 4.4 copy.80
  230.1 7.9 %fusion.24 = f32[256,3,32]{1,2,0:T(8,128)} fusion(f32[256,3,32]{1,2,0:T(8,128)} %copy.80, f32[256,32,3]{2,1,0:T(8,128)} %bitcast.183, pred[256,32]{1,0:T(8,128)(4,1)S(1)} %copy-done.15, pred[256,32]{1,0:T(8,128)(4,1)S(1)} %copy-done.13), kind=kOutput, calls=%fused_computation.52 | output fusion | flops 173630 | bytes 311296 | tf_op jit(solution)/shard_map/div | solution.py:38
  238.0 4.3 copy.103
  242.2 3.0 multiply_reduce_fusion.2
  245.2 1.0 convolution_convert_fusion.3
  246.4 1.2 reduce-window.6
  248.2 35.9 %all-reduce.13.cloned.1.call-done = bf16[256,768]{1,0:T(8,128)(2,1)} async-done(((bf16[256,768]{1,0:T(8,128)(2,1)}), bf16[256,768]{1,0:T(8,128)(2,1)}) %all-reduce.13.cloned.1.call-update) | async-done | bytes 393232 | tf_op jit(solution)/shard_map/psum | solution.py:89
  284.1 1.2 fusion.67
  285.3 1.5 convolution_convert_fusion.7
  286.8 2.9 multiply_reduce_fusion.1
  289.8 4.4 copy.92
  294.2 8.1 %fusion.25 = f32[256,3,32]{1,2,0:T(8,128)} fusion(f32[256,3,32]{1,2,0:T(8,128)} %copy.92, pred[256,32]{1,0:T(8,128)(4,1)S(1)} %copy-done.17), kind=kOutput, calls=%fused_computation.53 | output fusion | flops 149054 | bytes 204800 | tf_op jit(solution)/shard_map/div | solution.py:50
  302.3 3.6 copy.105
  306.0 2.7 multiply_reduce_fusion
  308.6 2.0 convolution_convert_fusion.2
  311.0 0.9 slice_reduce_fusion
  312.0 0.8 fusion.130
  312.8 35.7 %all-reduce.15.cloned.1.call-done = bf16[256,768]{1,0:T(8,128)(2,1)} async-done(((bf16[256,768]{1,0:T(8,128)(2,1)}), bf16[256,768]{1,0:T(8,128)(2,1)}) %all-reduce.15.cloned.1.call-update) | async-done | bytes 393232 | tf_op jit(solution)/shard_map/psum | solution.py:94
  348.5 1.3 fusion.71
  350.5 1.2 convolution_convert_fusion
  351.7 19.0 %all_to_all.36 = bf16[16,32,768]{2,1,0:T(8,128)(2,1)S(1)} all-to-all(bf16[16,32,768]{2,1,0:T(8,128)(2,1)S(1)} %convolution_convert_fusion), channel_id=1, replica_groups=mesh['dp'=1,'tp'=4,'ep'=8] {'ep'}, dimensions={0} | all-to-all | bytes 1572864 | tf_op jit(solution)/shard_map/all_to_all | solution.py:71
  370.8 1.9 fusion.168
  372.7 5.3 %convolution_convert_fusion.1 = bf16[2,256,768]{2,1,0:T(8,128)(2,1)} fusion(bf16[2,768,768]{2,1,0:T(8,128)(2,1)} %param.47, f32[2,256,768]{2,1,0:T(8,128)} %fusion.168, bf16[2,256,768]{2,1,0:T(8,128)(2,1)S(1)} %bitcast.162, bf16[2,768,768]{2,1,0:T(8,128)(2,1)} %param.46), kind=kOutput, calls=%fused_computation.64 | convolution fusion | flops 1212284928 | bytes 7864320 | tf_op jit(solution)/shard_map/ecf,efd->ecd/dot_general | solution.py:75
  378.0 9.3 %broadcast_select_fusion.1 = (bf16[1,256,3,32,64]{1,4,3,2,0:T(8,128)(2,1)}, bf16[1,256,3,32,64]{1,4,3,2,0:T(8,128)(2,1)}, bf16[1,256,3,32,64]{1,4,3,2,0:T(8,128)(2,1)}, bf16[1,256,3,32,64]{1,4,3,2,0:T(8,128)(2,1)}) fusion(pred[256,32]{0,1:T(8,128)(4,1)S(1)} %get-tuple-element.24, bf16[2,256,3,32,64]{1,4,3,2,0:T(8,128)(2,1)} %param.30, ...), kind=kLoop, calls=%fused_computation.42 | loop fusion | flops 6291456 | bytes 25567232 | tf_op jit(solution)/shard_map/jit(_where)/select_n | solution.py:34
  387.3 27.2 %all-reduce.17.cloned.1.call-done = bf16[2,256,768]{2,1,0:T(8,128)(2,1)} async-done(((bf16[2,256,768]{2,1,0:T(8,128)(2,1)}), bf16[2,256,768]{2,1,0:T(8,128)(2,1)}) %all-reduce.17.cloned.1.call-update) | async-done | bytes 786448 | tf_op jit(solution)/shard_map/psum | solution.py:76
  414.6 2.8 copy.48
  417.4 7.3 %all-to-all-start.1 = ((bf16[2,256,768]{2,0,1:T(2,128)(2,1)}), bf16[2,256,768]{2,0,1:T(2,128)(2,1)S(1)}, u32[]{:S(2)}, u32[]{:S(2)}) async-start(bf16[2,256,768]{2,0,1:T(2,128)(2,1)} %copy.48), calls=%async_computation.1 | async-start | bytes 1572864 | tf_op jit(solution)/shard_map/all_to_all | solution.py:77
  424.7 10.3 %pad_maximum_fusion = (bf16[2,256,3,32,64]{1,4,3,2,0:T(8,128)(2,1)}, bf16[2,256,3,32,64]{1,4,3,2,0:T(8,128)(2,1)}) fusion(bf16[1,256,3,32,64]{1,4,3,2,0:T(8,128)(2,1)} %get-tuple-element.20, bf16[1,256,3,32,64]{1,4,3,2,0:T(8,128)(2,1)} %get-tuple-element.21, bf16[1,256,3,32,64]{1,4,3,2,0:T(8,128)(2,1)} %get-tuple-element.17, ...), kind=kLoop, calls=%fused_computation.9 | loop fusion | flops 6291456 | bytes 25165824 | tf_op jit(solution)/shard_map/stack | solution.py:101
  435.4 1.2 all-to-all-done.1
  436.7 1.9 fusion.41
  (87 shorter events, 4.8 us)
Async XLA Ops:
  7.2 363.6 %copy-start = (bf16[2,768,768]{2,1,0:T(8,128)(2,1)S(1)}, bf16[2,768,768]{2,1,0:T(8,128)(2,1)}, u32[]{:S(2)}) copy-start(bf16[2,768,768]{2,1,0:T(8,128)(2,1)} %param.45) | copy-start | bytes 7077892
  7.2 100.3 %all-reduce.7.cloned.1.call-start = ((), (), s32[]{:S(2)}) async-start(), calls=%async_computation.2 | async-start | bytes 786432 | tf_op jit(solution)/shard_map/psum | solution.py:89
  12.3 40.5 %copy-start.12 = (pred[256,32]{1,0:T(8,128)(4,1)}, pred[256,32]{1,0:T(8,128)(4,1)S(1)}, u32[]{:S(2)}) copy-start(pred[256,32]{1,0:T(8,128)(4,1)S(1)} %copy.41) | copy-start | bytes 24580
  12.4 40.3 %copy-start.14 = (pred[256,32]{1,0:T(8,128)(4,1)}, pred[256,32]{1,0:T(8,128)(4,1)S(1)}, u32[]{:S(2)}) copy-start(pred[256,32]{1,0:T(8,128)(4,1)S(1)} %copy.42) | copy-start | bytes 24580
  14.1 3.0 copy-start.6
  15.6 48.7 %copy-start.8 = (bf16[256,192]{0,1:T(8,128)(2,1)}, bf16[256,192]{0,1:T(8,128)(2,1)S(1)}, u32[]{:S(2)}) copy-start(bf16[256,192]{0,1:T(8,128)(2,1)S(1)} %convolution_convert_fusion.12) | copy-start | bytes 294916
  60.6 6.6 %copy-start.4 = (bf16[2,192,768]{2,1,0:T(8,128)(2,1)S(1)}, bf16[2,192,768]{2,1,0:T(8,128)(2,1)}, u32[]{:S(2)}) copy-start(bf16[2,192,768]{2,1,0:T(8,128)(2,1)} %param.38) | copy-start | bytes 1769476
  60.6 46.9 %copy-start.1 = (bf16[256,768]{1,0:T(8,128)(2,1)S(1)}, bf16[256,768]{1,0:T(8,128)(2,1)}, u32[]{:S(2)}) copy-start(bf16[256,768]{1,0:T(8,128)(2,1)} %param.25) | copy-start | bytes 1179652
  68.4 103.4 %all-reduce.9.cloned.1.call-start = ((), (), s32[]{:S(2)}) async-start(), calls=%async_computation.3 | async-start | bytes 786432 | tf_op jit(solution)/shard_map/psum | solution.py:94
  69.5 48.1 %copy-start.16 = (pred[256,32]{1,0:T(8,128)(4,1)}, pred[256,32]{1,0:T(8,128)(4,1)S(1)}, u32[]{:S(2)}) copy-start(pred[256,32]{1,0:T(8,128)(4,1)S(1)} %copy.45) | copy-start | bytes 24580
  125.7 46.1 %copy-start.3 = (bf16[256,768]{1,0:T(8,128)(2,1)S(1)}, bf16[256,768]{1,0:T(8,128)(2,1)}, u32[]{:S(2)}) copy-start(bf16[256,768]{1,0:T(8,128)(2,1)} %all-reduce.7.cloned.1.call-done) | copy-start | bytes 1179652
  134.1 83.1 %all-reduce.11.cloned.1.call-start = ((), (), s32[]{:S(2)}) async-start(), calls=%async_computation.4 | async-start | bytes 786432 | tf_op jit(solution)/shard_map/psum | solution.py:98
  175.7 42.6 %copy-start.20 = (f32[768]{0:T(1024)S(1)}, f32[768]{0:T(1024)}, u32[]{:S(2)}) copy-start(f32[768]{0:T(1024)} %get-tuple-element.5) | copy-start | bytes 9220
  179.4 104.7 %all-reduce.13.cloned.1.call-start = ((), (), s32[]{:S(2)}) async-start(), calls=%async_computation.5 | async-start | bytes 786432 | tf_op jit(solution)/shard_map/psum | solution.py:89
  222.4 7.7 %copy-start.13 = (pred[256,32]{1,0:T(8,128)(4,1)S(1)}, pred[256,32]{1,0:T(8,128)(4,1)}, u32[]{:S(2)}) copy-start(pred[256,32]{1,0:T(8,128)(4,1)} %copy-done.12) | copy-start | bytes 24580
  222.4 7.7 %copy-start.15 = (pred[256,32]{1,0:T(8,128)(4,1)S(1)}, pred[256,32]{1,0:T(8,128)(4,1)}, u32[]{:S(2)}) copy-start(pred[256,32]{1,0:T(8,128)(4,1)} %copy-done.14) | copy-start | bytes 24580
  238.0 7.3 %copy-start.5 = (bf16[2,192,768]{2,1,0:T(8,128)(2,1)S(1)}, bf16[2,192,768]{2,1,0:T(8,128)(2,1)}, u32[]{:S(2)}) copy-start(bf16[2,192,768]{2,1,0:T(8,128)(2,1)} %param.38) | copy-start | bytes 1769476
  238.0 8.4 %copy-start.19 = (s32[256]{0:T(256)S(1)}, s32[256]{0:T(256)}, u32[]{:S(2)}) copy-start(s32[256]{0:T(256)} %param.28) | copy-start | bytes 3076
  246.3 102.1 %all-reduce.15.cloned.1.call-start = ((), (), s32[]{:S(2)}) async-start(), calls=%async_computation.6 | async-start | bytes 786432 | tf_op jit(solution)/shard_map/psum | solution.py:94
  286.8 7.4 %copy-start.17 = (pred[256,32]{1,0:T(8,128)(4,1)S(1)}, pred[256,32]{1,0:T(8,128)(4,1)}, u32[]{:S(2)}) copy-start(pred[256,32]{1,0:T(8,128)(4,1)} %copy-done.16) | copy-start | bytes 24580
  302.3 46.2 %copy-start.2 = (bf16[256,768]{1,0:T(8,128)(2,1)S(1)}, bf16[256,768]{1,0:T(8,128)(2,1)}, u32[]{:S(2)}) copy-start(bf16[256,768]{1,0:T(8,128)(2,1)} %all-reduce.13.cloned.1.call-done) | copy-start | bytes 1179652
  310.7 103.8 %all-reduce.17.cloned.1.call-start = ((), (), s32[]{:S(2)}) async-start(), calls=%async_computation.7 | async-start | bytes 1572864 | tf_op jit(solution)/shard_map/psum | solution.py:76
  312.8 57.9 %copy-start.18 = (s32[256,32]{0,1:T(8,128)}, s32[256,32]{0,1:T(8,128)S(1)}, u32[]{:S(2)}) copy-start(s32[256,32]{0,1:T(8,128)S(1)} %fusion.127) | copy-start | bytes 98308
  349.7 0.7 copy-start.10
  349.8 21.0 %copy-start.21 = (f32[256]{0:T(256)}, f32[256]{0:T(256)S(1)}, u32[]{:S(2)}) copy-start(f32[256]{0:T(256)S(1)} %add_rsqrt_fusion) | copy-start | bytes 3076
  372.7 5.3 %copy-start.7 = (bf16[256,192]{0,1:T(8,128)(2,1)S(1)}, bf16[256,192]{0,1:T(8,128)(2,1)}, u32[]{:S(2)}) copy-start(bf16[256,192]{0,1:T(8,128)(2,1)} %copy-done.6) | copy-start | bytes 294916
  372.7 5.3 %copy-start.9 = (bf16[256,192]{0,1:T(8,128)(2,1)S(1)}, bf16[256,192]{0,1:T(8,128)(2,1)}, u32[]{:S(2)}) copy-start(bf16[256,192]{0,1:T(8,128)(2,1)} %copy-done.8) | copy-start | bytes 294916
  417.4 19.3 %all-to-all-start.1 = ((bf16[2,256,768]{2,0,1:T(2,128)(2,1)}), bf16[2,256,768]{2,0,1:T(2,128)(2,1)S(1)}, u32[]{:S(2)}, u32[]{:S(2)}) async-start(bf16[2,256,768]{2,0,1:T(2,128)(2,1)} %copy.48), calls=%async_computation.1 | async-start | bytes 1572864 | tf_op jit(solution)/shard_map/all_to_all | solution.py:77
  424.7 10.3 %copy-start.11 = (bf16[256,768]{1,0:T(8,128)(2,1)S(1)}, bf16[256,768]{1,0:T(8,128)(2,1)}, u32[]{:S(2)}) copy-start(bf16[256,768]{1,0:T(8,128)(2,1)} %copy-done.10) | copy-start | bytes 1179652
  424.7 10.3 %copy-start.22 = (f32[256]{0:T(256)S(1)}, f32[256]{0:T(256)}, u32[]{:S(2)}) copy-start(f32[256]{0:T(256)} %copy-done.21) | copy-start | bytes 3076
  424.7 10.3 %copy-start.23 = (f32[768,16]{0,1:T(8,128)S(1)}, f32[768,16]{0,1:T(8,128)}, u32[]{:S(2)}) copy-start(f32[768,16]{0,1:T(8,128)} %param.44) | copy-start | bytes 147460
Sparse Core Ops, SparseCore 0:
  68.5 38.9 all-reduce.6
  134.2 37.5 all-reduce.8
  179.5 37.5 all-reduce.10
  246.5 37.6 all-reduce.12
  310.8 37.6 all-reduce.14
  378.1 36.3 all-reduce.16
where the time goes:
time: 448 us; the launch traced here: 446 us
  waiting for transfers between devices  213 us (48%)
  other arithmetic  87.6 us (20%)
  local copies, waits for them, and re-layouts  68.3 us (15%)
  matrix products  34.4 us (8%)
  blocking collectives  19 us (4%)
  between operations  14.5 us (3%)
  starting transfers between devices  8.34 us (2%)
    psum x2, waiting for transfers between devices, decode_body(): h_cur = add_residual(h_cur, lax.psum(attn_part.astype(jnp.bfloat16), 'tp'))  73.8 us
    psum x2, waiting for transfers between devices, decode_body(): h_cur = add_residual(h_cur, lax.psum(cross_part.astype(jnp.bfloat16), 'tp'))  73.3 us
    psum x1, waiting for transfers between devices, decode_body(): h_cur = add_residual(h_cur, lax.psum(ffn_part.astype(jnp.bfloat16), 'tp'))  37.5 us
    gather x1, local copies, waits for them, and re-layouts, self_attention(): bias = jnp.take(rel_bias, jnp.maximum(distance, 0), axis=1)  28 us
    psum x1, waiting for transfers between devices, switch_layer(): expert_out = lax.psum(expert_out, 'tp')  27.2 us
    dot_general x14, matrix products, project(): return jnp.dot(normed, weight, preferred_element_type=jnp.float32)  23.7 us
    all_to_all x1, blocking collectives, switch_layer(): received = lax.all_to_all(buffers, 'ep', 0, 1, tiled=True)  19 us
    unnamed x53, local copies, waits for them, and re-layouts  16.8 us
  transfers between devices with their start and end apart: 7, of which 7 were waited for; matrix products, arithmetic and copies ran while one was open for 5% of the time, Pallas kernels for 0%

commit v1 on v0

v1 whole, which is shorter than its diff:
```python
import functools

import jax
import jax.numpy as jnp
from jax import lax
from jax.experimental import pallas as pl
from jax.experimental.pallas import tpu as pltpu
from jax.sharding import PartitionSpec as P

EPS = 1e-6
NEG_BIG = -1e9
MESH = pl.DeviceIdType.MESH
LANES = 128
VMEM = pl.BlockSpec(memory_space=pltpu.VMEM)
ANY = pl.BlockSpec(memory_space=pl.ANY)
VMEM_LIMIT = 60 * 1024 * 1024

NT = (((1,), (1,)), ((), ()))
NN = (((1,), (0,)), ((), ()))
TN = (((0,), (0,)), ((), ()))


def dot(a, b, dims=NN, **kw):
    return lax.dot_general(a, b, dims, preferred_element_type=jnp.float32, **kw)


def rms_norm(h, scale):
    h = h.astype(jnp.float32)
    inv = lax.rsqrt(jnp.mean(h * h, axis=-1, keepdims=True) + EPS)
    return (h * inv * scale).astype(jnp.bfloat16)


def softmax_rows(s):
    p = jnp.exp(s - jnp.max(s, axis=0, keepdims=True))
    return (p / jnp.sum(p, axis=0, keepdims=True)).astype(jnp.bfloat16).astype(jnp.float32)


def slot_scores(query, load, slots):
    rows = [jnp.sum(load(j).astype(jnp.float32) * query, axis=0, keepdims=True) for j in range(slots)]
    return jnp.concatenate(rows, axis=0)


def self_kernel(layer, h_ref, scale_ref, pos_ref, bias_ref, wq_ref, wk_ref, wv_ref, k_ref, v_ref, *rest):
    ctx_ref, ko_ref, vo_ref, q_s, k_s, v_s, b_s = rest[-7:]
    heads, halves, dim, lanes = q_s.shape
    slots = k_ref.shape[2]
    step = pl.program_id(0)

    @pl.when(step == 0)
    def _():
        x = rms_norm(h_ref[...], scale_ref[...])
        qt = dot(wq_ref[...], x, NT).astype(jnp.bfloat16)
        kt = dot(wk_ref[...], x, NT).astype(jnp.bfloat16)
        vt = dot(wv_ref[...], x, NT).astype(jnp.bfloat16)
        tokens = x.shape[0]
        onehot = (lax.broadcasted_iota(jnp.int32, (LANES, tokens), 0) == pos_ref[...]).astype(jnp.float32)
        for a in range(heads):
            row = jnp.concatenate([bias_ref[a:a + 1, :], jnp.zeros((1, LANES - slots), jnp.float32)], axis=1)
            table = pltpu.roll(jnp.broadcast_to(row, (slots, LANES)), 0, 1, stride=1, stride_axis=0)
            bias = dot(table, onehot, precision=lax.Precision.HIGHEST)
            for b in range(halves):
                rs, cs = slice(a * dim, (a + 1) * dim), slice(b * lanes, (b + 1) * lanes)
                q_s[a, b] = qt[rs, cs].astype(jnp.float32)
                k_s[a, b] = kt[rs, cs]
                v_s[a, b] = vt[rs, cs]
                b_s[a, b] = bias[:, cs]

    head, half = step // halves, step % halves
    pos = pos_ref[:, pl.ds(pl.multiple_of(half * lanes, lanes), lanes)]
    pos_bf = jnp.broadcast_to(pos.astype(jnp.float32), (dim, lanes)).astype(jnp.bfloat16)
    query, k_new, v_new = q_s[head, half], k_s[head, half], v_s[head, half]
    slot_id = lax.broadcasted_iota(jnp.int32, (slots, lanes), 0)

    rows = []
    for j in range(slots):
        old = k_ref[0, 0, j]
        ko_ref[0, 0, j] = jnp.where(pos_bf == jnp.bfloat16(j), k_new, old)
        rows.append(jnp.sum(old.astype(jnp.float32) * query, axis=0, keepdims=True))
    scores = jnp.concatenate(rows, axis=0)
    new_score = jnp.sum(k_new.astype(jnp.float32) * query, axis=0, keepdims=True)
    at_slot = slot_id == pos
    scores = jnp.where(at_slot, new_score, scores)
    scores = jnp.where(slot_id <= pos, scores + b_s[head, half], NEG_BIG)
    prob = softmax_rows(scores)
    prob_new = jnp.sum(jnp.where(at_slot, prob, 0.0), axis=0, keepdims=True)
    prob_old = jnp.where(at_slot, 0.0, prob)
    acc = v_new.astype(jnp.float32) * prob_new
    for j in range(slots):
        old = v_ref[0, 0, j]
        vo_ref[0, 0, j] = jnp.where(pos_bf == jnp.bfloat16(j), v_new, old)
        acc += old.astype(jnp.float32) * prob_old[j:j + 1, :]
    ctx_ref[...] = acc.astype(jnp.bfloat16)


def self_attention(layer, h, scale, pos, rel_bias, wq, wk, wv, keys, values, prev):
    tokens, width = h.shape
    _, heads, slots, dim, _ = keys.shape
    halves = tokens // LANES
    cache = pl.BlockSpec((1, 1, slots, dim, LANES), lambda i: (layer, i // halves, 0, 0, i % halves))
    full = lambda a: pl.BlockSpec(a.shape, lambda i: (0,) * a.ndim)
    args = [h, scale, pos, rel_bias, wq, wk, wv, keys, values]
    specs = [full(a) for a in args[:7]] + [cache, cache]
    aliases = {}
    if prev is not None:
        aliases = {len(args): 1, len(args) + 1: 2}
        args += list(prev)
        specs += [ANY, ANY]
    return pl.pallas_call(
        functools.partial(self_kernel, layer),
        grid=(heads * halves,),
        out_shape=(jax.ShapeDtypeStruct((heads * dim, tokens), jnp.bfloat16), jax.ShapeDtypeStruct(keys.shape, keys.dtype), jax.ShapeDtypeStruct(values.shape, values.dtype)),
        in_specs=specs,
        out_specs=(pl.BlockSpec((dim, LANES), lambda i: (i // halves, i % halves)), cache, cache),
        scratch_shapes=[
            pltpu.VMEM((heads, halves, dim, LANES), jnp.float32),
            pltpu.VMEM((heads, halves, dim, LANES), jnp.bfloat16),
            pltpu.VMEM((heads, halves, dim, LANES), jnp.bfloat16),
            pltpu.VMEM((heads, halves, slots, LANES), jnp.float32),
        ],
        input_output_aliases=aliases,
        compiler_params=pltpu.CompilerParams(vmem_limit_bytes=VMEM_LIMIT, dimension_semantics=("arbitrary",)),
        name=f"self_attention_{layer}",
    )(*args)


def cross_attention(x, mask_ref, wq, k_buf, v_buf, ctx_s, q_s):
    heads, slots, dim, tokens = k_buf.shape
    halves = tokens // LANES
    qt = dot(wq, x, NT).astype(jnp.bfloat16)
    for a in range(heads):
        q_s[a] = qt[a * dim:(a + 1) * dim, :].astype(jnp.float32)

    def one_head(a, carry):
        for b in range(halves):
            cs = slice(b * LANES, (b + 1) * LANES)
            scores = slot_scores(q_s[a, :, cs], lambda j: k_buf[a, j, :, cs], slots)
            prob = softmax_rows(jnp.where(mask_ref[:, cs] > 0, scores, NEG_BIG))
            acc = jnp.zeros((dim, LANES), jnp.float32)
            for j in range(slots):
                acc += v_buf[a, j, :, cs].astype(jnp.float32) * prob[j:j + 1, :]
            ctx_s[a, :, cs] = acc.astype(jnp.bfloat16)
        return carry

    lax.fori_loop(0, heads, one_head, 0)
    return ctx_s[...].reshape(heads * dim, tokens)


def enter(peers):
    barrier = pltpu.get_barrier_semaphore()
    for axis, index in peers:
        pl.semaphore_signal(barrier, inc=1, device_id={axis: index}, device_id_type=MESH)
    pl.semaphore_wait(barrier, len(peers))


class Group:
    def __init__(self, axis, n, sems):
        self.axis, self.n, self.me = axis, n, lax.axis_index(axis)
        self.send, self.recv = sems

    def peer(self, k):
        return lax.rem(self.me + k, self.n)

    def peers(self):
        return [(self.axis, self.peer(k)) for k in range(1, self.n)]

    def exchange(self, phase, src, dst):
        copies = []
        for k in range(1, self.n):
            copy = pltpu.make_async_remote_copy(
                src_ref=src(k, self.peer(k)),
                dst_ref=dst(k, self.peer(k)),
                send_sem=self.send.at[phase, k - 1],
                recv_sem=self.recv.at[phase, k - 1],
                device_id={self.axis: self.peer(k)},
                device_id_type=MESH,
            )
            copy.start()
            copies.append(copy)
        return copies


def sum_over_tp(tp, phase, part, part_s, in_s, h_ref, out_s, gate_ref=None):
    tokens = part.shape[0]
    rows = tokens // tp.n
    part_s[...] = part.astype(jnp.bfloat16)
    block = lambda i: pl.ds(pl.multiple_of(i * rows, rows), rows)
    copies = tp.exchange(2 * phase, lambda k, i: part_s.at[block(i)], lambda k, i: in_s.at[phase, k - 1])
    total = part_s[block(tp.me), :].astype(jnp.float32)
    for k, copy in enumerate(copies):
        copy.wait_recv()
        total += in_s[phase, k].astype(jnp.float32)
    total = total.astype(jnp.bfloat16).astype(jnp.float32)
    if gate_ref is not None:
        total = total * gate_ref[block(tp.me), :]
    out_s[block(tp.me), :] = (h_ref[block(tp.me), :].astype(jnp.float32) + total).astype(jnp.bfloat16)
    mine = out_s.at[block(tp.me)]
    spread = tp.exchange(2 * phase + 1, lambda k, i: mine, lambda k, i: mine)
    for copy in spread:
        copy.wait_recv()
    return copies + spread


def gelu_product(gate, up):
    return (jax.nn.gelu(gate) * up).astype(jnp.bfloat16)


def loader(sems):
    pending = {}

    def start(name, src, dst):
        copy = pltpu.make_async_copy(src, dst, sems.at[len(pending)])
        copy.start()
        pending[name] = copy

    return start, pending


def dense_kernel(n_tp, layer, h_ref, ctx_ref, scale_ref, mask_ref, wo_ref, wcq_ref, wco_ref, wg_ref, wu_ref, wd_ref, ck_ref, cv_ref, out_ref,
                 k_buf, v_buf, wo, wcq, wco, wg, wu, wd, q_s, ctx_s, part_s, in_s, h1, h2, load_sem, tp_send, tp_recv):
    start, pending = loader(load_sem)
    start("wo", wo_ref.at[layer], wo)
    start("wcq", wcq_ref.at[layer], wcq)
    start("ck", ck_ref.at[layer], k_buf)
    start("cv", cv_ref.at[layer], v_buf)
    start("wco", wco_ref.at[layer], wco)
    start("wg", wg_ref, wg)
    start("wu", wu_ref, wu)
    start("wd", wd_ref, wd)
    tp = Group("tp", n_tp, (tp_send, tp_recv))
    enter(tp.peers())

    pending["wo"].wait()
    sent = sum_over_tp(tp, 0, dot(ctx_ref[...], wo[...], TN), part_s.at[0], in_s, h_ref, h1)
    x = rms_norm(h1[...], scale_ref[1:2, :])
    for name in ("wcq", "ck", "cv", "wco"):
        pending[name].wait()
    ctx = cross_attention(x, mask_ref, wcq[...], k_buf, v_buf, ctx_s, q_s)
    sent += sum_over_tp(tp, 1, dot(ctx, wco[...], TN), part_s.at[1], in_s, h1, h2)
    x = rms_norm(h2[...], scale_ref[2:3, :])
    for name in ("wg", "wu", "wd"):
        pending[name].wait()
    product = gelu_product(dot(x, wg[...]), dot(x, wu[...]))
    sent += sum_over_tp(tp, 2, dot(product, wd[...]), part_s.at[2], in_s, h2, out_ref)
    for copy in sent:
        copy.wait_send()


def dense_block(n_tp, layer, h, ctx, scale, mask, w_out, w_cq, w_co, w_gate, w_up, w_down, cross_k, cross_v):
    tokens, width = h.shape
    _, heads, slots, dim, _ = cross_k.shape
    rows = tokens // n_tp
    bf = lambda *s: pltpu.VMEM(s, jnp.bfloat16)
    return pl.pallas_call(
        functools.partial(dense_kernel, n_tp, layer),
        out_shape=jax.ShapeDtypeStruct(h.shape, h.dtype),
        in_specs=[VMEM] * 4 + [ANY] * 8,
        out_specs=VMEM,
        scratch_shapes=[
            bf(*cross_k.shape[1:]), bf(*cross_v.shape[1:]), bf(*w_out.shape[1:]), bf(*w_cq.shape[1:]), bf(*w_co.shape[1:]),
            bf(*w_gate.shape), bf(*w_up.shape), bf(*w_down.shape),
            pltpu.VMEM((heads, dim, tokens), jnp.float32), bf(heads, dim, tokens),
            bf(3, tokens, width), bf(3, n_tp - 1, rows, width), bf(tokens, width), bf(tokens, width),
            pltpu.SemaphoreType.DMA((8,)), pltpu.SemaphoreType.DMA((6, n_tp - 1)), pltpu.SemaphoreType.DMA((6, n_tp - 1)),
        ],
        compiler_params=pltpu.CompilerParams(vmem_limit_bytes=VMEM_LIMIT, collective_id=0, has_side_effects=True),
        name="block_a",
    )(h, ctx, scale, mask, w_out, w_cq, w_co, w_gate, w_up, w_down, cross_k, cross_v)


def routing(idx_row, idx_col, experts):
    tokens = idx_row.shape[1]
    capacity = (2 * tokens + experts - 1) // experts
    one_t = lax.broadcasted_iota(jnp.int32, (experts, tokens), 0) == idx_row
    one = lax.broadcasted_iota(jnp.int32, (tokens, experts), 1) == idx_col
    earlier = lax.broadcasted_iota(jnp.int32, (tokens, tokens), 0) < lax.broadcasted_iota(jnp.int32, (tokens, tokens), 1)
    later = lax.broadcasted_iota(jnp.int32, (tokens, tokens), 0) > lax.broadcasted_iota(jnp.int32, (tokens, tokens), 1)
    to_bf = lambda m: m.astype(jnp.float32).astype(jnp.bfloat16)
    count_t = dot(to_bf(one_t), to_bf(earlier))
    count = dot(to_bf(later), to_bf(one))
    slot_row = jnp.sum(jnp.where(one_t, count_t, 0.0), axis=0, keepdims=True)
    slot_col = jnp.sum(jnp.where(one, count, 0.0), axis=1, keepdims=True)
    place = lambda slot, idx: jnp.where(slot < capacity, idx.astype(jnp.float32) * capacity + slot, -1.0)
    return place(slot_row, idx_row), place(slot_col, idx_col), one, capacity


def moe_kernel(n_tp, n_ep, layer, h_ref, ctx_ref, scale_ref, mask_ref, idx_row_ref, idx_col_ref, router_ref, wo_ref, wcq_ref, wco_ref, wg_ref, wu_ref, wd_ref, ck_ref, cv_ref, out_ref,
               k_buf, v_buf, wo, wcq, wco, wg, wu, wd, q_s, ctx_s, part_s, in_s, h1, h2, disp, x_in, y_out, y_in, gate_s, load_sem, tp_send, tp_recv, ep_send, ep_recv):
    start, pending = loader(load_sem)
    start("wo", wo_ref.at[layer], wo)
    start("wcq", wcq_ref.at[layer], wcq)
    start("ck", ck_ref.at[layer], k_buf)
    start("cv", cv_ref.at[layer], v_buf)
    start("wco", wco_ref.at[layer], wco)
    start("wg", wg_ref, wg)
    start("wu", wu_ref, wu)
    start("wd", wd_ref, wd)
    tp = Group("tp", n_tp, (tp_send, tp_recv))
    ep = Group("ep", n_ep, (ep_send, ep_recv))
    enter(tp.peers() + ep.peers())

    pending["wo"].wait()
    sent = sum_over_tp(tp, 0, dot(ctx_ref[...], wo[...], TN), part_s.at[0], in_s, h_ref, h1)
    x = rms_norm(h1[...], scale_ref[1:2, :])
    for name in ("wcq", "ck", "cv", "wco"):
        pending[name].wait()
    ctx = cross_attention(x, mask_ref, wcq[...], k_buf, v_buf, ctx_s, q_s)
    sent += sum_over_tp(tp, 1, dot(ctx, wco[...], TN), part_s.at[1], in_s, h1, h2)

    x = rms_norm(h2[...], scale_ref[2:3, :])
    tokens, width = x.shape
    experts = router_ref.shape[0]
    local = experts // n_ep
    place_row, place_col, one, capacity = routing(idx_row_ref[...], idx_col_ref[...], experts)
    spots = experts * capacity
    to_bf = lambda m: m.astype(jnp.float32).astype(jnp.bfloat16)
    pick = to_bf(lax.broadcasted_iota(jnp.int32, (spots, tokens), 0).astype(jnp.float32) == place_row)
    disp[...] = dot(pick, x).astype(jnp.bfloat16).reshape(disp.shape)
    x_in[ep.me] = disp[ep.me]
    there = ep.exchange(0, lambda k, i: disp.at[i], lambda k, i: x_in.at[ep.me])
    logits = dot(x.astype(jnp.float32), router_ref[...], NT, precision=lax.Precision.HIGHEST)
    prob = jnp.exp(logits - jnp.max(logits, axis=1, keepdims=True))
    prob = prob / jnp.sum(prob, axis=1, keepdims=True)
    gate_s[...] = jnp.sum(jnp.where(one, prob, 0.0), axis=1, keepdims=True)
    for name in ("wg", "wu", "wd"):
        pending[name].wait()
    for copy in there:
        copy.wait_recv()
    for j in range(local):
        rows = x_in[:, j].reshape(n_ep * capacity, width)
        product = gelu_product(dot(rows, wg[j]), dot(rows, wu[j]))
        y_out[:, j] = dot(product, wd[j]).astype(jnp.bfloat16).reshape(n_ep, capacity, width)
    y_in[ep.me] = y_out[ep.me]
    back = ep.exchange(1, lambda k, i: y_out.at[i], lambda k, i: y_in.at[ep.me])
    put = to_bf(lax.broadcasted_iota(jnp.int32, (tokens, spots), 1).astype(jnp.float32) == place_col)
    for copy in back:
        copy.wait_recv()
    part = dot(put, y_in[...].reshape(spots, width))
    sent += sum_over_tp(tp, 2, part, part_s.at[2], in_s, h2, out_ref, gate_s)
    for copy in sent + there + back:
        copy.wait_send()


def moe_block(n_tp, n_ep, layer, h, ctx, scale, mask, idx_row, idx_col, router, w_out, w_cq, w_co, w_gate, w_up, w_down, cross_k, cross_v):
    tokens, width = h.shape
    _, heads, slots, dim, _ = cross_k.shape
    rows = tokens // n_tp
    experts = router.shape[0]
    capacity = (2 * tokens + experts - 1) // experts
    bf = lambda *s: pltpu.VMEM(s, jnp.bfloat16)
    spots = (n_ep, experts // n_ep, capacity, width)
    return pl.pallas_call(
        functools.partial(moe_kernel, n_tp, n_ep, layer),
        out_shape=jax.ShapeDtypeStruct(h.shape, h.dtype),
        in_specs=[VMEM] * 7 + [ANY] * 8,
        out_specs=VMEM,
        scratch_shapes=[
            bf(*cross_k.shape[1:]), bf(*cross_v.shape[1:]), bf(*w_out.shape[1:]), bf(*w_cq.shape[1:]), bf(*w_co.shape[1:]),
            bf(*w_gate.shape), bf(*w_up.shape), bf(*w_down.shape),
            pltpu.VMEM((heads, dim, tokens), jnp.float32), bf(heads, dim, tokens),
            bf(3, tokens, width), bf(3, n_tp - 1, rows, width), bf(tokens, width), bf(tokens, width),
            bf(*spots), bf(*spots), bf(*spots), bf(*spots), pltpu.VMEM((tokens, 1), jnp.float32),
            pltpu.SemaphoreType.DMA((8,)), pltpu.SemaphoreType.DMA((6, n_tp - 1)), pltpu.SemaphoreType.DMA((6, n_tp - 1)),
            pltpu.SemaphoreType.DMA((2, n_ep - 1)), pltpu.SemaphoreType.DMA((2, n_ep - 1)),
        ],
        compiler_params=pltpu.CompilerParams(vmem_limit_bytes=VMEM_LIMIT, collective_id=1, has_side_effects=True),
        name="block_b",
    )(h, ctx, scale, mask, idx_row, idx_col, router, w_out, w_cq, w_co, w_gate, w_up, w_down, cross_k, cross_v)


def decode_body(n_tp, n_ep, hidden, write_pos, enc_mask, expert_idx, self_keys, self_values, cross_keys, cross_values, rel_bias, norm_scale, w_query, w_key, w_value, w_out, w_cross_query, w_cross_out, dense_gate, dense_up, dense_down, router, exp_gate, exp_up, exp_down):
    lanes = lambda c: jnp.transpose(c, (0, 2, 3, 4, 1))
    sk, sv, ck, cv = lanes(self_keys), lanes(self_values), lanes(cross_keys), lanes(cross_values)
    flip = lambda w: jnp.swapaxes(w, 1, 2)
    wq, wk, wv, wcq = flip(w_query), flip(w_key), flip(w_value), flip(w_cross_query)
    pos = write_pos[None, :]
    mask = enc_mask.T
    caches = None
    h = hidden
    for layer in range(2):
        ctx, *caches = self_attention(layer, h, norm_scale[layer, 0:1], pos, rel_bias, wq[layer], wk[layer], wv[layer], sk, sv, caches)
        if layer == 0:
            h = dense_block(n_tp, layer, h, ctx, norm_scale[layer], mask, w_out, wcq, w_cross_out, dense_gate, dense_up, dense_down, ck, cv)
        else:
            h = moe_block(n_tp, n_ep, layer, h, ctx, norm_scale[layer], mask, expert_idx[None, :], expert_idx[:, None], router.T, w_out, wcq, w_cross_out, exp_gate, exp_up, exp_down, ck, cv)
    back = lambda c: jnp.transpose(c, (0, 4, 1, 2, 3))
    return h, back(caches[0]), back(caches[1])


def solution(mesh):
    batch = ('dp', 'ep')
    row_spec = P(batch, None)
    vec_spec = P(batch)
    cache_spec = P(None, batch, 'tp', None, None)
    col_spec = P(None, None, 'tp')
    out_rows = P(None, 'tp', None)
    in_specs = (row_spec, vec_spec, row_spec, vec_spec, cache_spec, cache_spec, cache_spec, cache_spec, P('tp', None), P(), col_spec, col_spec, col_spec, out_rows, col_spec, out_rows, P(None, 'tp'), P(None, 'tp'), P('tp', None), P(), P('ep', None, 'tp'), P('ep', None, 'tp'), P('ep', 'tp', None))
    out_specs = (row_spec, cache_spec, cache_spec)
    body = functools.partial(decode_body, mesh.shape['tp'], mesh.shape['ep'])
    return jax.shard_map(body, mesh=mesh, in_specs=in_specs, out_specs=out_specs, check_vma=False)
```

time: 448 us -> 145 us (0.32)
  waiting for transfers between devices: 213 us -> 0 us
  Pallas kernels: 0 us -> 135 us
  other arithmetic: 87.6 us -> 0 us
  local copies, waits for them, and re-layouts: 68.3 us -> 8.77 us
  matrix products: 34.4 us -> 0 us
  blocking collectives: 19 us -> 0 us
  between operations: 14.5 us -> 0.67 us
  starting transfers between devices: 8.34 us -> 0 us
    psum x6 -> x0, waiting for transfers between devices: 212 us -> none  [the longest x2 73.8 us: decode_body(): h_cur = add_residual(h_cur, lax.psum(attn_part.astype(jnp.bfloat16), 'tp'))]
    pallas_call x0 -> x4, Pallas kernels: none -> 135 us  [the longest x1 73.2 us: moe_block(): pl.pallas_call(functools.partial(moe_kernel, n_tp, n_ep, layer), out_shap...]
    dot_general x19 -> x0, matrix products: 34.4 us -> none  [the longest x14 23.7 us: project(): return jnp.dot(normed, weight, preferred_element_type=jnp.float32)]
    div x4 -> x0, other arithmetic: 32 us -> none  [the longest x2 16.3 us: cross_attention(): attn_prob = jax.nn.softmax(scores, axis=-1).astype(jnp.bfloat16)]
    gather x1 -> x0, local copies, waits for them, and re-layouts: 28 us -> none  [self_attention(): bias = jnp.take(rel_bias, jnp.maximum(distance, 0), axis=1)]
    all_to_all x1 -> x0, blocking collectives: 19 us -> none  [switch_layer(): received = lax.all_to_all(buffers, 'ep', 0, 1, tiled=True)]
    dot_general x4 -> x0, local copies, waits for them, and re-layouts: 17.7 us -> none  [the longest x2 8.85 us: cross_attention(): jnp.einsum('thd,thsd->ths', query, keys, preferred_element_type=jnp.float32)]
    unnamed x53 -> x5, local copies, waits for them, and re-layouts: 16.8 us -> 1.78 us
  transfers between devices with their start and end apart: 7 -> 0, of which waited for: 7 -> 0; matrix products, arithmetic and copies ran while one was open for 5% -> 0% of each run, Pallas kernels for 0% -> 0%
where the time goes in v1:
time: 145 us; the launch traced here: 144 us
  Pallas kernels  135 us (93%)
  local copies, waits for them, and re-layouts  8.77 us (6%)
    pallas_call x1, Pallas kernels, moe_block(): pl.pallas_call(functools.partial(moe_kernel, n_tp, n_ep, layer), out_shap...  73.2 us
    pallas_call x1, Pallas kernels, dense_block(): pl.pallas_call(functools.partial(dense_kernel, n_tp, layer), out_shape=ja...  44.9 us
    pallas_call x2, Pallas kernels, self_attention(): pl.pallas_call(functools.partial(self_kernel, layer), grid=(heads * halve...  16.8 us

profile of v1, /device:TPU:97, one launch (start us, length us, event | category | flops | bytes accessed | tf_op | source)
XLA Modules:
  0.0 144.3 jit_solution(18344154872822145618)
XLA Ops:
  0.6 2.3 %slice_bitcast_fusion = (bf16[192,768]{1,0:T(8,128)(2,1)}, bf16[192,768]{1,0:T(8,128)(2,1)}, bf16[192,768]{1,0:T(8,128)(2,1)}, bf16[192,768]{1,0:T(8,128)(2,1)}) fusion(bf16[2,192,768]{2,1,0:T(8,128)(2,1)} %bitcast.48, bf16[2,192,768]{2,1,0:T(8,128)(2,1)} %bitcast.49), kind=kLoop, calls=%fused_computation | loop fusion | bytes 2359296 | tf_op jit(solution)/shard_map/squeeze | solution.py:380
  2.9 1.9 %slice_bitcast_fusion.2 = (bf16[192,768]{1,0:T(8,128)(2,1)}, bf16[192,768]{1,0:T(8,128)(2,1)}) fusion(bf16[2,192,768]{2,1,0:T(8,128)(2,1)} %bitcast.47), kind=kLoop, calls=%fused_computation.2 | loop fusion | bytes 1179648 | tf_op jit(solution)/shard_map/squeeze | solution.py:380
  4.8 1.4 slice_bitcast_fusion.6
  6.2 0.0 copy-start
  6.2 8.4 %self_attention_0.1 = (bf16[192,256]{1,0:T(8,128)(2,1)}, bf16[2,3,32,64,256]{4,3,2,1,0:T(8,128)(2,1)}, bf16[2,3,32,64,256]{4,3,2,1,0:T(8,128)(2,1)}) custom-call(bf16[256,768]{1,0:T(8,128)(2,1)} %h_ref.3, f32[1,768]{1,0:T(1,128)} %get-tuple-element.24.scale_ref, s32[1,256]{1,0:T(1,128)} %bitcast.53, f32[3,32]{1,0:T(4,128)} %bias_ref.3, ...), custom_call_target="tpu_custom_call" | custom-call | tf_op jit(solution)/shard_map/self_attention_0/pallas_call | solution.py:108
  14.6 0.0 copy-done
  14.6 0.6 copy_bitcast_fusion
  15.2 44.9 %block_a.1.h_ref = bf16[256,768]{1,0:T(8,128)(2,1)} custom-call(bf16[256,768]{1,0:T(8,128)(2,1)} %h_ref.3, bf16[192,256]{1,0:T(8,128)(2,1)} %get-tuple-element.9.ctx_ref, f32[3,768]{1,0:T(4,128)} %get-tuple-element.28.scale_ref, s32[32,256]{1,0:T(8,128)} %bitcast.50, bf16[2,192,768]{2,1,0:T(8,128)(2,1)} %wo_ref.3, bf16[2,192,768]{2,1,0:T(8,128)(2,1)} %bitcast.45, ...), custom_call_target="tpu_custom_call" | custom-call | tf_op jit(solution)/shard_map/block_a/pallas_call | solution.py:253
  60.1 0.0 copy-start.1
  60.1 8.4 %self_attention_1.1 = (bf16[192,256]{1,0:T(8,128)(2,1)}, bf16[2,3,32,64,256]{4,3,2,1,0:T(8,128)(2,1)}, bf16[2,3,32,64,256]{4,3,2,1,0:T(8,128)(2,1)}) custom-call(bf16[256,768]{1,0:T(8,128)(2,1)} %block_a.1.h_ref, f32[1,768]{1,0:T(1,128)} %get-tuple-element.23.scale_ref, s32[1,256]{1,0:T(1,128)} %bitcast.54, ...), custom_call_target="tpu_custom_call", output_to_operand_aliasing={{1}: (9, {}), {2}: (10, {})} | custom-call | tf_op jit(solution)/shard_map/self_attention_1/pallas_call | solution.py:108
  68.5 0.0 copy-done.1
  68.5 0.8 copy.32.idx_col_ref
  69.3 73.2 %block_b.1 = bf16[256,768]{1,0:T(8,128)(2,1)} custom-call(bf16[256,768]{1,0:T(8,128)(2,1)} %block_a.1.h_ref, bf16[192,256]{1,0:T(8,128)(2,1)} %get-tuple-element.12.ctx_ref, f32[3,768]{1,0:T(4,128)} %get-tuple-element.27.scale_ref, s32[32,256]{1,0:T(8,128)} %bitcast.51, s32[1,256]{1,0:T(1,128)} %bitcast.55, s32[256,1]{1,0:T(8,128)} %copy.32.idx_col_ref, ...), custom_call_target="tpu_custom_call" | custom-call | tf_op jit(solution)/shard_map/block_b/pallas_call | solution.py:351
  142.5 1.8 %copy.40 = bf16[256,768]{1,0:T(8,128)(2,1)} copy(bf16[256,768]{1,0:T(8,128)(2,1)} %block_b.1) | data formatting | bytes 786432
  (1 shorter events, 0.0 us)
Async XLA Ops:
  6.2 8.4 %copy-start = (f32[2,3,768]{2,0,1:T(2,128)S(1)}, f32[2,3,768]{2,0,1:T(2,128)}, u32[]{:S(2)}) copy-start(f32[2,3,768]{2,0,1:T(2,128)} %param.32) | copy-start | bytes 55300
  60.1 8.4 %copy-start.1 = (s32[256]{0:T(256)S(1)}, s32[256]{0:T(256)}, u32[]{:S(2)}) copy-start(s32[256]{0:T(256)} %param.26) | copy-start | bytes 3076

commit v2 on v0

v2 whole, which is shorter than its diff:
```python
import functools

import jax
import jax.numpy as jnp
from jax import lax
from jax.experimental import pallas as pl
from jax.experimental.pallas import tpu as pltpu
from jax.sharding import PartitionSpec as P

EPS = 1e-6
NEG_BIG = -1e9
MESH = pl.DeviceIdType.MESH
LANES = 128
VMEM = pl.BlockSpec(memory_space=pltpu.VMEM)
ANY = pl.BlockSpec(memory_space=pl.ANY)
VMEM_LIMIT = 48 * 1024 * 1024
OUT = pltpu.VMEM

NT = (((1,), (1,)), ((), ()))
NN = (((1,), (0,)), ((), ()))
TN = (((0,), (0,)), ((), ()))


def dot(a, b, dims=NN, **kw):
    return lax.dot_general(a, b, dims, preferred_element_type=jnp.float32, **kw)


def rms_norm(h, scale):
    h = h.astype(jnp.float32)
    inv = lax.rsqrt(jnp.mean(h * h, axis=-1, keepdims=True) + EPS)
    return (h * inv * scale).astype(jnp.bfloat16)


def softmax_rows(s):
    p = jnp.exp(s - jnp.max(s, axis=0, keepdims=True))
    return (p / jnp.sum(p, axis=0, keepdims=True)).astype(jnp.bfloat16).astype(jnp.float32)


def to_bf(mask):
    return mask.astype(jnp.float32).astype(jnp.bfloat16)


def enter(peers):
    barrier = pltpu.get_barrier_semaphore()
    for axis, index in peers:
        pl.semaphore_signal(barrier, inc=1, device_id={axis: index}, device_id_type=MESH)
    pl.semaphore_wait(barrier, len(peers))


def remote(src, dst, send_sem, recv_sem, device):
    copy = pltpu.make_async_remote_copy(src_ref=src, dst_ref=dst, send_sem=send_sem, recv_sem=recv_sem, device_id=device, device_id_type=MESH)
    copy.start()
    return copy


class Group:
    def __init__(self, axis, n, send, recv):
        self.axis, self.n, self.me = axis, n, lax.axis_index(axis)
        self.send, self.recv = send, recv

    def peer(self, k):
        return lax.rem(self.me + k, self.n)

    def peers(self):
        return [(self.axis, self.peer(k)) for k in range(1, self.n)]

    def copy_to(self, phase, k, src, dst):
        return remote(src, dst, self.send.at[phase, k - 1], self.recv.at[phase, k - 1], {self.axis: self.peer(k)})


class Spread:
    def __init__(self, slot, tp, ep, shard, full, send, recv):
        self.slot, self.tp, self.ep, self.shard, self.full, self.send, self.recv = slot, tp, ep, shard, full, send, recv
        rows, cols = shard.shape
        self.far = ep.n // 2
        self.half, self.place = lax.rem(ep.me, 2), ep.me // 2
        height, width = rows // self.far, cols // 2
        self.rows = pl.ds(pl.multiple_of(self.place * height, 16), height)
        self.cols = pl.ds(pl.multiple_of(self.half * width, LANES), width)
        self.copies, self.used = [], 0

    def _copy(self, src, dst, device):
        i = self.used
        self.used += 1
        copy = remote(src, dst, self.send.at[self.slot, i], self.recv.at[self.slot, i], device)
        self.copies.append(copy)
        return copy

    def over_tp(self):
        tp = self.tp
        self.first = [self._copy(self.shard.at[self.rows, self.cols], self.full.at[tp.me, self.rows, self.cols], {tp.axis: tp.peer(k)}) for k in range(1, tp.n)]

    def along_ep(self):
        for copy in self.first:
            copy.wait_recv()
        tp, ep = self.tp, self.ep
        self.second = []
        for m in range(1, self.far):
            there = lax.rem(self.place + m, self.far) * 2 + self.half
            for k in range(1, tp.n):
                piece = self.full.at[tp.peer(k), self.rows, self.cols]
                self.second.append(self._copy(piece, piece, {ep.axis: there}))

    def to_neighbour(self):
        for copy in self.second:
            copy.wait_recv()
        tp, ep = self.tp, self.ep
        there = self.place * 2 + 1 - self.half
        self.third = []
        for k in range(1, tp.n):
            piece = self.full.at[tp.peer(k), :, self.cols]
            self.third.append(self._copy(piece, piece, {ep.axis: there}))

    def finish(self):
        for copy in self.third:
            copy.wait_recv()


def routing(idx_row, experts):
    tokens = idx_row.shape[1]
    capacity = (2 * tokens + experts - 1) // experts
    one_t = lax.broadcasted_iota(jnp.int32, (experts, tokens), 0) == idx_row
    earlier = lax.broadcasted_iota(jnp.int32, (tokens, tokens), 0) < lax.broadcasted_iota(jnp.int32, (tokens, tokens), 1)
    count = dot(to_bf(one_t), to_bf(earlier))
    slot = jnp.sum(jnp.where(one_t, count, 0.0), axis=0, keepdims=True)
    place = jnp.where(slot < capacity, idx_row.astype(jnp.float32) * capacity + slot, -1.0)
    return place, one_t, capacity


def gelu_product(gate, up):
    return (jax.nn.gelu(gate) * up).astype(jnp.bfloat16)


def block_kernel(n_tp, n_ep, h_ref, scale_ref, pos_ref, mask_ref, bias_ref, idx_ref, router_ref,
                 wq_ref, wk_ref, wv_ref, wcq_ref, wo_ref, wco_ref, dg_ref, du_ref, dd_ref, eg_ref, eu_ref, ed_ref, sk_ref, sv_ref, ck_ref, cv_ref,
                 out_ref, ko_ref, vo_ref,
                 ck_buf, cv_buf, w_in, w_full, dg, du, dd, eg, eu, ed,
                 q_s, k_s, v_s, b_s, ctx_s, part_s, in_s, prod_s, h_s, disp, x_in, y_out, y_in, gate_s,
                 load_sem, cache_sem, tp_send, tp_recv, ctx_send, ctx_recv, ep_send, ep_recv, w_send, w_recv):
    heads, slots, dim, tokens = sk_ref.shape[1:]
    width = h_ref.shape[1]
    halves = tokens // LANES
    rows = tokens // n_tp
    tp = Group("tp", n_tp, tp_send, tp_recv)
    ep = Group("ep", n_ep, ep_send, ep_recv)
    sent = []

    pending = {}

    def load(name, src, dst):
        copy = pltpu.make_async_copy(src, dst, load_sem.at[len(pending)])
        copy.start()
        pending[name] = copy

    def ready(*names):
        for name in names:
            pending[name].wait()

    def cache_copies(which, layer, a):
        src = (sk_ref, sv_ref, ck_ref, cv_ref)[which].at[layer, a]
        dst = (ko_ref, vo_ref, ck_buf, cv_buf)[which].at[layer, a]
        return pltpu.make_async_copy(src, dst, cache_sem.at[which, layer, a])

    def load_caches(first, layer):
        for a in range(heads):
            cache_copies(first, layer, a).start()
            cache_copies(first + 1, layer, a).start()

    for i, ref in enumerate((wq_ref, wk_ref, wv_ref)):
        load(("w", 0, i), ref.at[0], w_in.at[0, i])
    load_caches(0, 0)
    enter(tp.peers() + ep.peers())

    spreads = [Spread(2 * layer + i, tp, ep, ref.at[layer], w_full.at[2 * layer + i], w_send, w_recv) for layer in range(2) for i, ref in enumerate((wo_ref, wco_ref))]
    spreads[0].over_tp()
    load(("full", 0), wo_ref.at[0], w_full.at[0, tp.me])
    load(("w", 0, 3), wcq_ref.at[0], w_in.at[0, 3])

    onehot = (lax.broadcasted_iota(jnp.int32, (LANES, tokens), 0) == pos_ref[...]).astype(jnp.float32)
    for a in range(heads):
        row = jnp.concatenate([bias_ref[a:a + 1, :], jnp.zeros((1, LANES - slots), jnp.float32)], axis=1)
        table = pltpu.roll(jnp.broadcast_to(row, (slots, LANES)), 0, 1, stride=1, stride_axis=0)
        b_s[a] = dot(table, onehot, precision=lax.Precision.HIGHEST)
    slot_id = lax.broadcasted_iota(jnp.int32, (slots, LANES), 0)

    def weighted(v_buf, a, cs, prob, acc):
        for j in range(slots):
            acc += v_buf[a, j, :, cs].astype(jnp.float32) * prob[j:j + 1, :]
        return acc

    def send_context(sub, a):
        mine = ctx_s.at[sub, tp.me, a]
        for k in range(1, n_tp):
            remote(mine, mine, ctx_send.at[sub, a, k - 1], ctx_recv.at[sub, a, k - 1], {"tp": tp.peer(k)})

    def context_copies(sub):
        mine = lambda a: ctx_s.at[sub, tp.me, a]
        return [pltpu.make_async_remote_copy(src_ref=mine(a), dst_ref=mine(a), send_sem=ctx_send.at[sub, a, k - 1], recv_sem=ctx_recv.at[sub, a, k - 1], device_id={"tp": tp.peer(k)}, device_id_type=MESH)
                for a in range(heads) for k in range(1, n_tp)]

    def out_project(sub, h, out):
        copies = context_copies(sub)
        for copy in copies:
            copy.wait_recv()
        spreads[sub].finish()
        ready(("full", sub))
        result = dot(ctx_s[sub].reshape(n_tp * heads * dim, tokens), w_full[sub].reshape(n_tp * heads * dim, width), TN)
        out[...] = (h[...].astype(jnp.float32) + result.astype(jnp.bfloat16).astype(jnp.float32)).astype(jnp.bfloat16)
        sent.extend(copies)

    def self_attention(layer, h, between=None):
        x = rms_norm(h[...], scale_ref[0, layer:layer + 1, :])
        ready(*[("w", layer, i) for i in range(3)])
        qt, kt, vt = (dot(w_in[layer, i], x, NT).astype(jnp.bfloat16) for i in range(3))
        for a in range(heads):
            q_s[a] = qt[a * dim:(a + 1) * dim, :].astype(jnp.float32)
            k_s[a] = kt[a * dim:(a + 1) * dim, :]
            v_s[a] = vt[a * dim:(a + 1) * dim, :]
        kb, vb = ko_ref.at[layer], vo_ref.at[layer]
        sub = 2 * layer

        def one_head(a, carry):
            cache_copies(0, layer, a).wait()
            cache_copies(1, layer, a).wait()
            for b in range(halves):
                cs = slice(b * LANES, (b + 1) * LANES)
                pos = pos_ref[:, cs]
                pos_bf = jnp.broadcast_to(pos.astype(jnp.float32), (dim, LANES)).astype(jnp.bfloat16)
                query, k_new, v_new = q_s[a, :, cs], k_s[a, :, cs], v_s[a, :, cs]
                parts = []
                for j in range(slots):
                    old = kb[a, j, :, cs]
                    kb[a, j, :, cs] = jnp.where(pos_bf == jnp.bfloat16(j), k_new, old)
                    parts.append(jnp.sum(old.astype(jnp.float32) * query, axis=0, keepdims=True))
                scores = jnp.concatenate(parts, axis=0)
                at_slot = slot_id == pos
                scores = jnp.where(at_slot, jnp.sum(k_new.astype(jnp.float32) * query, axis=0, keepdims=True), scores)
                prob = softmax_rows(jnp.where(slot_id <= pos, scores + b_s[a, :, cs], NEG_BIG))
                prob_new = jnp.sum(jnp.where(at_slot, prob, 0.0), axis=0, keepdims=True)
                prob_old = jnp.where(at_slot, 0.0, prob)
                acc = v_new.astype(jnp.float32) * prob_new
                for j in range(slots):
                    old = vb[a, j, :, cs]
                    vb[a, j, :, cs] = jnp.where(pos_bf == jnp.bfloat16(j), v_new, old)
                    acc += old.astype(jnp.float32) * prob_old[j:j + 1, :]
                ctx_s[sub, tp.me, a, :, cs] = acc.astype(jnp.bfloat16)
            send_context(sub, a)
            return carry

        lax.fori_loop(0, heads, one_head, 0)

    def cross_attention(layer, h):
        x = rms_norm(h[...], scale_ref[1, layer:layer + 1, :])
        ready(("w", layer, 3))
        qt = dot(w_in[layer, 3], x, NT).astype(jnp.bfloat16)
        for a in range(heads):
            q_s[a] = qt[a * dim:(a + 1) * dim, :].astype(jnp.float32)
        kb, vb = ck_buf.at[layer], cv_buf.at[layer]
        sub = 2 * layer + 1

        def one_head(a, carry):
            cache_copies(2, layer, a).wait()
            cache_copies(3, layer, a).wait()
            for b in range(halves):
                cs = slice(b * LANES, (b + 1) * LANES)
                query = q_s[a, :, cs]
                scores = jnp.concatenate([jnp.sum(kb[a, j, :, cs].astype(jnp.float32) * query, axis=0, keepdims=True) for j in range(slots)], axis=0)
                prob = softmax_rows(jnp.where(mask_ref[:, cs] > 0, scores, NEG_BIG))
                ctx_s[sub, tp.me, a, :, cs] = weighted(vb, a, cs, prob, jnp.zeros((dim, LANES), jnp.float32)).astype(jnp.bfloat16)
            send_context(sub, a)
            return carry

        lax.fori_loop(0, heads, one_head, 0)

    block = lambda i: pl.ds(pl.multiple_of(i * rows, rows), rows)

    def sum_over_tp(phase, part, h, out, gate=None):
        for k in (2, 1, 3)[:n_tp - 1] if n_tp == 4 else range(1, n_tp):
            part_s[phase, k] = part(tp.peer(k)).astype(jnp.bfloat16)
            sent.append(tp.copy_to(2 * phase, k, part_s.at[phase, k], in_s.at[phase, k - 1]))
        copies = sent[-(n_tp - 1):]
        total = part(tp.me)
        for copy in copies:
            copy.wait_recv()
        for k in range(n_tp - 1):
            total += in_s[phase, k].astype(jnp.float32)
        total = total.astype(jnp.bfloat16).astype(jnp.float32)
        if gate is not None:
            total = total * gate[block(tp.me), :]
        out[block(tp.me), :] = (h[block(tp.me), :].astype(jnp.float32) + total).astype(jnp.bfloat16)
        mine = out.at[block(tp.me)]
        copies = [tp.copy_to(2 * phase + 1, k, mine, mine) for k in range(1, n_tp)]
        for copy in copies:
            copy.wait_recv()
        sent.extend(copies)

    self_attention(0, h_ref)
    spreads[0].along_ep()
    spreads[1].over_tp()
    load(("full", 1), wco_ref.at[0], w_full.at[1, tp.me])
    load_caches(2, 0)
    for i, (name, ref, dst) in enumerate((("dg", dg_ref, dg), ("du", du_ref, du), ("dd", dd_ref, dd))):
        load(name, ref, dst)
    for i, ref in enumerate((wq_ref, wk_ref, wv_ref, wcq_ref)):
        load(("w", 1, i), ref.at[1], w_in.at[1, i])
    spreads[0].to_neighbour()
    spreads[1].along_ep()
    out_project(0, h_ref, h_s.at[0])
    for s in (2, 3):
        spreads[s].over_tp()
    load(("full", 2), wo_ref.at[1], w_full.at[2, tp.me])
    load(("full", 3), wco_ref.at[1], w_full.at[3, tp.me])
    load_caches(0, 1)
    cross_attention(0, h_s.at[0])
    spreads[1].to_neighbour()
    spreads[2].along_ep()
    out_project(1, h_s.at[0], h_s.at[1])
    load_caches(2, 1)
    for name, ref, dst in (("eg", eg_ref, eg), ("eu", eu_ref, eu), ("ed", ed_ref, ed)):
        load(name, ref, dst)
    x = rms_norm(h_s[1], scale_ref[2, 0:1, :])
    ready("dg", "du", "dd")
    prod_s[...] = gelu_product(dot(x, dg[...]), dot(x, du[...]))
    sum_over_tp(0, lambda i: dot(prod_s[block(i), :], dd[...]), h_s.at[1], h_s.at[2])
    spreads[2].to_neighbour()
    spreads[3].along_ep()

    self_attention(1, h_s.at[2])
    spreads[3].to_neighbour()
    out_project(2, h_s.at[2], h_s.at[3])
    cross_attention(1, h_s.at[3])
    experts = router_ref.shape[0]
    local = experts // n_ep
    place, one_t, capacity = routing(idx_ref[...], experts)
    spots = experts * capacity
    out_project(3, h_s.at[3], h_s.at[4])
    x = rms_norm(h_s[4], scale_ref[2, 1:2, :])
    pick = to_bf(lax.broadcasted_iota(jnp.int32, (spots, tokens), 0).astype(jnp.float32) == place)
    disp[...] = dot(pick, x).astype(jnp.bfloat16).reshape(disp.shape)
    there = [[ep.copy_to(j, k, disp.at[ep.peer(k), j], x_in.at[j, ep.me]) for k in range(1, n_ep)] for j in range(local)]
    logits = dot(router_ref[...], x.astype(jnp.float32), NT, precision=lax.Precision.HIGHEST)
    prob = jnp.exp(logits - jnp.max(logits, axis=0, keepdims=True))
    prob = prob / jnp.sum(prob, axis=0, keepdims=True)
    gate = jnp.sum(jnp.where(one_t, prob, 0.0), axis=0, keepdims=True)
    turned = jnp.concatenate([gate, place, jnp.zeros((LANES - 2, tokens), jnp.float32)], axis=0).T
    gate_s[...] = turned[:, 0:1]
    put = to_bf(lax.broadcasted_iota(jnp.int32, (tokens, spots), 1).astype(jnp.float32) == turned[:, 1:2])
    ready("eg", "eu", "ed")
    back = []
    for j in range(local):
        x_in[j, ep.me] = disp[ep.me, j]
        for copy in there[j]:
            copy.wait_recv()
        own = x_in[j].reshape(n_ep * capacity, width)
        product = gelu_product(dot(own, eg[j]), dot(own, eu[j]))
        y_out[:, j] = dot(product, ed[j]).astype(jnp.bfloat16).reshape(n_ep, capacity, width)
        y_in[ep.me, j] = y_out[ep.me, j]
        back += [ep.copy_to(local + j, k, y_out.at[ep.peer(k), j], y_in.at[ep.me, j]) for k in range(1, n_ep)]
    for copy in back:
        copy.wait_recv()
    prod_s[...] = dot(put, y_in[...].reshape(spots, width)).astype(jnp.bfloat16)
    sum_over_tp(1, lambda i: prod_s[block(i), :].astype(jnp.float32), h_s.at[4], out_ref, gate_s)
    for copy in sent + sum(there, []) + back:
        copy.wait_send()
    for spread in spreads:
        for copy in spread.copies:
            copy.wait_send()


def two_blocks(n_tp, n_ep, h, scale, pos, mask, bias, idx, router, weights, dense, expert, caches):
    tokens, width = h.shape
    sk, ck = caches[0], caches[2]
    _, heads, slots, dim, _ = sk.shape
    rows = tokens // n_tp
    experts = router.shape[0]
    local = experts // n_ep
    capacity = (2 * tokens + experts - 1) // experts
    bf = lambda *s: pltpu.VMEM(s, jnp.bfloat16)
    f32 = lambda *s: pltpu.VMEM(s, jnp.float32)
    dma = lambda *s: pltpu.SemaphoreType.DMA(s)
    shard = weights[-1].shape[1]
    pieces = 2 * (n_tp - 1) + (n_ep // 2 - 1) * (n_tp - 1)
    spots = (n_ep, local, capacity, width)
    return pl.pallas_call(
        functools.partial(block_kernel, n_tp, n_ep),
        out_shape=(OUT(h.shape, h.dtype), OUT(sk.shape, sk.dtype), OUT(sk.shape, sk.dtype)),
        in_specs=[VMEM] * 7 + [ANY] * 16,
        out_specs=(VMEM, VMEM, VMEM),
        scratch_shapes=[
            bf(*ck.shape), bf(*ck.shape), bf(2, 4, heads * dim, width), bf(4, n_tp, shard, width),
            *[bf(*w.shape) for w in dense], *[bf(*w.shape) for w in expert],
            f32(heads, dim, tokens), bf(heads, dim, tokens), bf(heads, dim, tokens), f32(heads, slots, tokens),
            bf(4, n_tp, heads, dim, tokens), bf(2, n_tp, rows, width), bf(2, n_tp - 1, rows, width), bf(tokens, width), bf(5, tokens, width),
            bf(*spots), bf(local, n_ep, capacity, width), bf(*spots), bf(*spots), f32(tokens, 1),
            dma(18), dma(4, 2, heads), dma(4, n_tp - 1), dma(4, n_tp - 1), dma(4, heads, n_tp - 1), dma(4, heads, n_tp - 1),
            dma(2 * local, n_ep - 1), dma(2 * local, n_ep - 1), dma(4, pieces), dma(4, pieces),
        ],
        compiler_params=pltpu.CompilerParams(vmem_limit_bytes=VMEM_LIMIT, collective_id=0, has_side_effects=True),
        name="two_blocks",
    )(h, scale, pos, mask, bias, idx, router, *weights, *dense, *expert, *caches)


def decode_body(n_tp, n_ep, hidden, write_pos, enc_mask, expert_idx, self_keys, self_values, cross_keys, cross_values, rel_bias, norm_scale, w_query, w_key, w_value, w_out, w_cross_query, w_cross_out, dense_gate, dense_up, dense_down, router, exp_gate, exp_up, exp_down):
    caches = [jnp.transpose(c, (0, 2, 3, 4, 1)) for c in (self_keys, self_values, cross_keys, cross_values)]
    flip = lambda w: jnp.swapaxes(w, 1, 2)
    weights = (flip(w_query), flip(w_key), flip(w_value), flip(w_cross_query), w_out, w_cross_out)
    h, keys, values = two_blocks(n_tp, n_ep, hidden, jnp.swapaxes(norm_scale, 0, 1), write_pos[None, :], enc_mask.T, rel_bias, expert_idx[None, :], router.T,
                                 weights, (dense_gate, dense_up, dense_down), (exp_gate, exp_up, exp_down), caches)
    back = lambda c: jnp.transpose(c, (0, 4, 1, 2, 3))
    return h, back(keys), back(values)


def solution(mesh):
    batch = ('dp', 'ep')
    row_spec = P(batch, None)
    vec_spec = P(batch)
    cache_spec = P(None, batch, 'tp', None, None)
    col_spec = P(None, None, 'tp')
    out_rows = P(None, 'tp', None)
    in_specs = (row_spec, vec_spec, row_spec, vec_spec, cache_spec, cache_spec, cache_spec, cache_spec, P('tp', None), P(), col_spec, col_spec, col_spec, out_rows, col_spec, out_rows, P(None, 'tp'), P(None, 'tp'), P('tp', None), P(), P('ep', None, 'tp'), P('ep', None, 'tp'), P('ep', 'tp', None))
    out_specs = (row_spec, cache_spec, cache_spec)
    body = functools.partial(decode_body, mesh.shape['tp'], mesh.shape['ep'])
    return jax.shard_map(body, mesh=mesh, in_specs=in_specs, out_specs=out_specs, check_vma=False)
```

time: 448 us -> 106 us (0.24)
  waiting for transfers between devices: 213 us -> 0 us
  Pallas kernels: 0 us -> 99.2 us
  other arithmetic: 87.6 us -> 0 us
  local copies, waits for them, and re-layouts: 68.3 us -> 6.15 us
  matrix products: 34.4 us -> 0 us
  blocking collectives: 19 us -> 0 us
  between operations: 14.5 us -> 0.65 us
  starting transfers between devices: 8.34 us -> 0 us
    psum x6 -> x0, waiting for transfers between devices: 212 us -> none  [the longest x2 73.8 us: decode_body(): h_cur = add_residual(h_cur, lax.psum(attn_part.astype(jnp.bfloat16), 'tp'))]
    pallas_call x0 -> x1, Pallas kernels: none -> 99.2 us  [two_blocks(): pl.pallas_call(functools.partial(block_kernel, n_tp, n_ep), out_shape=(OU...]
    dot_general x19 -> x0, matrix products: 34.4 us -> none  [the longest x14 23.7 us: project(): return jnp.dot(normed, weight, preferred_element_type=jnp.float32)]
    div x4 -> x0, other arithmetic: 32 us -> none  [the longest x2 16.3 us: cross_attention(): attn_prob = jax.nn.softmax(scores, axis=-1).astype(jnp.bfloat16)]
    gather x1 -> x0, local copies, waits for them, and re-layouts: 28 us -> none  [self_attention(): bias = jnp.take(rel_bias, jnp.maximum(distance, 0), axis=1)]
    all_to_all x1 -> x0, blocking collectives: 19 us -> none  [switch_layer(): received = lax.all_to_all(buffers, 'ep', 0, 1, tiled=True)]
    dot_general x4 -> x0, local copies, waits for them, and re-layouts: 17.7 us -> none  [the longest x2 8.85 us: cross_attention(): jnp.einsum('thd,thsd->ths', query, keys, preferred_element_type=jnp.float32)]
    unnamed x8 -> x0, other arithmetic: 12.4 us -> none
  transfers between devices with their start and end apart: 7 -> 0, of which waited for: 7 -> 0; matrix products, arithmetic and copies ran while one was open for 5% -> 0% of each run, Pallas kernels for 0% -> 0%
where the time goes in v2:
time: 106 us
  Pallas kernels  99.2 us (94%)
  local copies, waits for them, and re-layouts  6.15 us (6%)
    pallas_call x1, Pallas kernels, two_blocks(): pl.pallas_call(functools.partial(block_kernel, n_tp, n_ep), out_shape=(OU...  99.2 us
    unnamed x3, local copies, waits for them, and re-layouts  6.15 us

profile of v2, /device:TPU:97, one launch (start us, length us, event | category | flops | bytes accessed | tf_op | source)
XLA Modules:
  0.0 106.0 jit_solution(13656131687038826799)
XLA Ops:
  0.6 99.2 %two_blocks.1 = (bf16[256,768]{1,0:T(8,128)(2,1)S(1)}, bf16[2,3,32,64,256]{4,3,2,1,0:T(8,128)(2,1)S(1)}, bf16[2,3,32,64,256]{4,3,2,1,0:T(8,128)(2,1)S(1)}) custom-call(bf16[256,768]{1,0:T(8,128)(2,1)} %h_ref.1, f32[3,2,768]{2,1,0:T(2,128)} %bitcast.27, s32[1,256]{1,0:T(1,128)} %bitcast.28, s32[32,256]{1,0:T(8,128)} %bitcast.26, f32[3,32]{1,0:T(4,128)} %bias_ref.1, ...), custom_call_target="tpu_custom_call" | custom-call | tf_op jit(solution)/shard_map/two_blocks/pallas_call | solution.py:384
  99.9 0.7 copy.29
  100.6 2.7 %copy.30 = bf16[2,256,3,32,64]{1,4,3,2,0:T(8,128)(2,1)} copy(bf16[2,256,3,32,64]{1,4,3,2,0:T(8,128)(2,1)S(1)} %bitcast.16) | data formatting | bytes 12582912
  103.3 2.7 %copy.31 = bf16[2,256,3,32,64]{1,4,3,2,0:T(8,128)(2,1)} copy(bf16[2,256,3,32,64]{1,4,3,2,0:T(8,128)(2,1)S(1)} %bitcast.15) | data formatting | bytes 12582912

commit v3 on v2

--- a/solution.py
+++ b/solution.py
@@ -15,6 +15,8 @@
 ANY = pl.BlockSpec(memory_space=pl.ANY)
 VMEM_LIMIT = 48 * 1024 * 1024
 OUT = pltpu.VMEM
+CHUNK = 256
+DIRECT = 64
 
 NT = (((1,), (1,)), ((), ()))
 NN = (((1,), (0,)), ((), ()))
@@ -40,11 +42,9 @@
     return mask.astype(jnp.float32).astype(jnp.bfloat16)
 
 
-def enter(peers):
-    barrier = pltpu.get_barrier_semaphore()
+def greet(peers):
     for axis, index in peers:
-        pl.semaphore_signal(barrier, inc=1, device_id={axis: index}, device_id_type=MESH)
-    pl.semaphore_wait(barrier, len(peers))
+        pl.semaphore_signal(pltpu.get_barrier_semaphore(), inc=1, device_id={axis: index}, device_id_type=MESH)
 
 
 def remote(src, dst, send_sem, recv_sem, device):
@@ -69,12 +69,14 @@
 
 
 class Spread:
-    def __init__(self, slot, tp, ep, shard, full, send, recv):
+    def __init__(self, slot, tp, ep, shard, full, send, recv, direct=0):
         self.slot, self.tp, self.ep, self.shard, self.full, self.send, self.recv = slot, tp, ep, shard, full, send, recv
         rows, cols = shard.shape
         self.far = ep.n // 2
         self.half, self.place = lax.rem(ep.me, 2), ep.me // 2
+        self.direct, rows = direct, rows - direct
         height, width = rows // self.far, cols // 2
+        self.rest = slice(rows, rows + direct)
         self.rows = pl.ds(pl.multiple_of(self.place * height, 16), height)
         self.cols = pl.ds(pl.multiple_of(self.half * width, LANES), width)
         self.copies, self.used = [], 0
@@ -89,6 +91,9 @@
     def over_tp(self):
         tp = self.tp
         self.first = [self._copy(self.shard.at[self.rows, self.cols], self.full.at[tp.me, self.rows, self.cols], {tp.axis: tp.peer(k)}) for k in range(1, tp.n)]
+        self.extra = []
+        if self.direct:
+            self.extra = [self._copy(self.shard.at[self.rest, self.cols], self.full.at[tp.me, self.rest, self.cols], {tp.axis: tp.peer(k)}) for k in range(1, tp.n)]
 
     def along_ep(self):
         for copy in self.first:
@@ -102,7 +107,7 @@
                 self.second.append(self._copy(piece, piece, {ep.axis: there}))
 
     def to_neighbour(self):
-        for copy in self.second:
+        for copy in self.second + self.extra:
             copy.wait_recv()
         tp, ep = self.tp, self.ep
         there = self.place * 2 + 1 - self.half
@@ -131,18 +136,20 @@
     return (jax.nn.gelu(gate) * up).astype(jnp.bfloat16)
 
 
-def block_kernel(n_tp, n_ep, h_ref, scale_ref, pos_ref, mask_ref, bias_ref, idx_ref, router_ref,
-                 wq_ref, wk_ref, wv_ref, wcq_ref, wo_ref, wco_ref, dg_ref, du_ref, dd_ref, eg_ref, eu_ref, ed_ref, sk_ref, sv_ref, ck_ref, cv_ref,
+def block_kernel(n_tp, n_ep, *refs):
+    small, (h_ref, scale_ref, pos_ref, mask_ref, bias_ref, idx_ref, router_ref), refs = refs[:7], refs[-7:], refs[7:-7]
+    (wq_ref, wk_ref, wv_ref, wcq_ref, wo_ref, wco_ref, dg_ref, du_ref, dd_ref, eg_ref, eu_ref, ed_ref, sk_ref, sv_ref, ck_ref, cv_ref,
                  out_ref, ko_ref, vo_ref,
                  ck_buf, cv_buf, w_in, w_full, dg, du, dd, eg, eu, ed,
                  q_s, k_s, v_s, b_s, ctx_s, part_s, in_s, prod_s, h_s, disp, x_in, y_out, y_in, gate_s,
-                 load_sem, cache_sem, tp_send, tp_recv, ctx_send, ctx_recv, ep_send, ep_recv, w_send, w_recv):
+                 load_sem, cache_sem, tp_send, tp_recv, ctx_send, ctx_recv, ep_send, ep_recv, w_send, w_recv) = refs
     heads, slots, dim, tokens = sk_ref.shape[1:]
     width = h_ref.shape[1]
     halves = tokens // LANES
     rows = tokens // n_tp
     tp = Group("tp", n_tp, tp_send, tp_recv)
     ep = Group("ep", n_ep, ep_send, ep_recv)
+    greet(tp.peers() + ep.peers())
     sent = []
 
     pending = {}
@@ -166,16 +173,19 @@
             cache_copies(first, layer, a).start()
             cache_copies(first + 1, layer, a).start()
 
+    for i, (src, dst) in enumerate(zip(small, (h_ref, scale_ref, pos_ref, mask_ref, bias_ref, idx_ref, router_ref))):
+        load(("small", i), src, dst)
     for i, ref in enumerate((wq_ref, wk_ref, wv_ref)):
         load(("w", 0, i), ref.at[0], w_in.at[0, i])
     load_caches(0, 0)
-    enter(tp.peers() + ep.peers())
-
-    spreads = [Spread(2 * layer + i, tp, ep, ref.at[layer], w_full.at[2 * layer + i], w_send, w_recv) for layer in range(2) for i, ref in enumerate((wo_ref, wco_ref))]
+    pl.semaphore_wait(pltpu.get_barrier_semaphore(), n_tp + n_ep - 2)
+
+    spreads = [Spread(2 * layer + i, tp, ep, ref.at[layer], w_full.at[2 * layer + i], w_send, w_recv, 0 if layer + i else DIRECT) for layer in range(2) for i, ref in enumerate((wo_ref, wco_ref))]
     spreads[0].over_tp()
     load(("full", 0), wo_ref.at[0], w_full.at[0, tp.me])
     load(("w", 0, 3), wcq_ref.at[0], w_in.at[0, 3])
 
+    ready(*[("small", i) for i in range(7)])
     onehot = (lax.broadcasted_iota(jnp.int32, (LANES, tokens), 0) == pos_ref[...]).astype(jnp.float32)
     for a in range(heads):
         row = jnp.concatenate([bias_ref[a:a + 1, :], jnp.zeros((1, LANES - slots), jnp.float32)], axis=1)
@@ -188,15 +198,16 @@
             acc += v_buf[a, j, :, cs].astype(jnp.float32) * prob[j:j + 1, :]
         return acc
 
-    def send_context(sub, a):
-        mine = ctx_s.at[sub, tp.me, a]
+    def context_copy(sub, a, b, k):
+        mine = ctx_s.at[sub, tp.me, a, :, pl.ds(b * LANES, LANES)]
+        return pltpu.make_async_remote_copy(src_ref=mine, dst_ref=mine, send_sem=ctx_send.at[sub, a, b, k - 1], recv_sem=ctx_recv.at[sub, a, b, k - 1], device_id={"tp": tp.peer(k)}, device_id_type=MESH)
+
+    def send_context(sub, a, b):
         for k in range(1, n_tp):
-            remote(mine, mine, ctx_send.at[sub, a, k - 1], ctx_recv.at[sub, a, k - 1], {"tp": tp.peer(k)})
+            context_copy(sub, a, b, k).start()
 
     def context_copies(sub):
-        mine = lambda a: ctx_s.at[sub, tp.me, a]
-        return [pltpu.make_async_remote_copy(src_ref=mine(a), dst_ref=mine(a), send_sem=ctx_send.at[sub, a, k - 1], recv_sem=ctx_recv.at[sub, a, k - 1], device_id={"tp": tp.peer(k)}, device_id_type=MESH)
-                for a in range(heads) for k in range(1, n_tp)]
+        return [context_copy(sub, a, b, k) for a in range(heads) for b in range(halves) for k in range(1, n_tp)]
 
     def out_project(sub, h, out):
         copies = context_copies(sub)
@@ -244,7 +255,7 @@
                     vb[a, j, :, cs] = jnp.where(pos_bf == jnp.bfloat16(j), v_new, old)
                     acc += old.astype(jnp.float32) * prob_old[j:j + 1, :]
                 ctx_s[sub, tp.me, a, :, cs] = acc.astype(jnp.bfloat16)
-            send_context(sub, a)
+                send_context(sub, a, b)
             return carry
 
         lax.fori_loop(0, heads, one_head, 0)
@@ -267,47 +278,55 @@
                 scores = jnp.concatenate([jnp.sum(kb[a, j, :, cs].astype(jnp.float32) * query, axis=0, keepdims=True) for j in range(slots)], axis=0)
                 prob = softmax_rows(jnp.where(mask_ref[:, cs] > 0, scores, NEG_BIG))
                 ctx_s[sub, tp.me, a, :, cs] = weighted(vb, a, cs, prob, jnp.zeros((dim, LANES), jnp.float32)).astype(jnp.bfloat16)
-            send_context(sub, a)
+                send_context(sub, a, b)
             return carry
 
         lax.fori_loop(0, heads, one_head, 0)
 
     block = lambda i: pl.ds(pl.multiple_of(i * rows, rows), rows)
 
-    def sum_over_tp(phase, part, h, out, gate=None):
-        for k in (2, 1, 3)[:n_tp - 1] if n_tp == 4 else range(1, n_tp):
-            part_s[phase, k] = part(tp.peer(k)).astype(jnp.bfloat16)
-            sent.append(tp.copy_to(2 * phase, k, part_s.at[phase, k], in_s.at[phase, k - 1]))
-        copies = sent[-(n_tp - 1):]
-        total = part(tp.me)
-        for copy in copies:
-            copy.wait_recv()
-        for k in range(n_tp - 1):
-            total += in_s[phase, k].astype(jnp.float32)
-        total = total.astype(jnp.bfloat16).astype(jnp.float32)
-        if gate is not None:
-            total = total * gate[block(tp.me), :]
-        out[block(tp.me), :] = (h[block(tp.me), :].astype(jnp.float32) + total).astype(jnp.bfloat16)
-        mine = out.at[block(tp.me)]
-        copies = [tp.copy_to(2 * phase + 1, k, mine, mine) for k in range(1, n_tp)]
-        for copy in copies:
-            copy.wait_recv()
-        sent.extend(copies)
+    col = lambda c: slice(c * CHUNK, (c + 1) * CHUNK)
+    chunks = width // CHUNK
+    order = [n_tp // 2] + [k for k in range(1, n_tp) if k != n_tp // 2]
+
+    def sum_over_tp(phase, prepare, part, h, out, gate=None, between=lambda: None):
+        gathers, spreads_out = [], []
+        for c in range(chunks):
+            prepare(c)
+            for k in order:
+                part_s[phase, c, k] = part(tp.peer(k), c).astype(jnp.bfloat16)
+                gathers.append(tp.copy_to((2 * phase) * chunks + c, k, part_s.at[phase, c, k], in_s.at[phase, c, k - 1]))
+        own = [part(tp.me, c) for c in range(chunks)]
+        between()
+        for c in range(chunks):
+            for copy in gathers[c * (n_tp - 1):(c + 1) * (n_tp - 1)]:
+                copy.wait_recv()
+            total = own[c]
+            for k in range(n_tp - 1):
+                total += in_s[phase, c, k].astype(jnp.float32)
+            total = total.astype(jnp.bfloat16).astype(jnp.float32)
+            if gate is not None:
+                total = total * gate[block(tp.me), :]
+            out[block(tp.me), col(c)] = (h[block(tp.me), col(c)].astype(jnp.float32) + total).astype(jnp.bfloat16)
+            mine = out.at[block(tp.me), col(c)]
+            spreads_out += [tp.copy_to((2 * phase + 1) * chunks + c, k, mine, mine) for k in order]
+        for copy in spreads_out:
+            copy.wait_recv()
+        sent.extend(gathers + spreads_out)
 
     self_attention(0, h_ref)
     spreads[0].along_ep()
-    spreads[1].over_tp()
+    for n in (1, 2, 3):
+        spreads[n].over_tp()
     load(("full", 1), wco_ref.at[0], w_full.at[1, tp.me])
     load_caches(2, 0)
-    for i, (name, ref, dst) in enumerate((("dg", dg_ref, dg), ("du", du_ref, du), ("dd", dd_ref, dd))):
+    for name, ref, dst in (("dg", dg_ref, dg), ("du", du_ref, du), ("dd", dd_ref, dd)):
         load(name, ref, dst)
     for i, ref in enumerate((wq_ref, wk_ref, wv_ref, wcq_ref)):
         load(("w", 1, i), ref.at[1], w_in.at[1, i])
     spreads[0].to_neighbour()
     spreads[1].along_ep()
     out_project(0, h_ref, h_s.at[0])
-    for s in (2, 3):
-        spreads[s].over_tp()
     load(("full", 2), wo_ref.at[1], w_full.at[2, tp.me])
     load(("full", 3), wco_ref.at[1], w_full.at[3, tp.me])
     load_caches(0, 1)
@@ -321,9 +340,12 @@
     x = rms_norm(h_s[1], scale_ref[2, 0:1, :])
     ready("dg", "du", "dd")
     prod_s[...] = gelu_product(dot(x, dg[...]), dot(x, du[...]))
-    sum_over_tp(0, lambda i: dot(prod_s[block(i), :], dd[...]), h_s.at[1], h_s.at[2])
-    spreads[2].to_neighbour()
-    spreads[3].along_ep()
+
+    def move_weights():
+        spreads[2].to_neighbour()
+        spreads[3].along_ep()
+
+    sum_over_tp(0, lambda c: None, lambda i, c: dot(prod_s[block(i), :], dd[:, col(c)]), h_s.at[1], h_s.at[2], between=move_weights)
 
     self_attention(1, h_s.at[2])
     spreads[3].to_neighbour()
@@ -346,20 +368,26 @@
     gate_s[...] = turned[:, 0:1]
     put = to_bf(lax.broadcasted_iota(jnp.int32, (tokens, spots), 1).astype(jnp.float32) == turned[:, 1:2])
     ready("eg", "eu", "ed")
-    back = []
+    back = {}
     for j in range(local):
         x_in[j, ep.me] = disp[ep.me, j]
         for copy in there[j]:
             copy.wait_recv()
         own = x_in[j].reshape(n_ep * capacity, width)
         product = gelu_product(dot(own, eg[j]), dot(own, eu[j]))
-        y_out[:, j] = dot(product, ed[j]).astype(jnp.bfloat16).reshape(n_ep, capacity, width)
-        y_in[ep.me, j] = y_out[ep.me, j]
-        back += [ep.copy_to(local + j, k, y_out.at[ep.peer(k), j], y_in.at[ep.me, j]) for k in range(1, n_ep)]
-    for copy in back:
-        copy.wait_recv()
-    prod_s[...] = dot(put, y_in[...].reshape(spots, width)).astype(jnp.bfloat16)
-    sum_over_tp(1, lambda i: prod_s[block(i), :].astype(jnp.float32), h_s.at[4], out_ref, gate_s)
+        for c in range(chunks):
+            y_out[c, :, j] = dot(product, ed[j, :, col(c)]).astype(jnp.bfloat16).reshape(n_ep, capacity, CHUNK)
+            y_in[c, ep.me, j] = y_out[c, ep.me, j]
+            back[j, c] = [ep.copy_to(local + j * chunks + c, k, y_out.at[c, ep.peer(k), j], y_in.at[c, ep.me, j]) for k in range(1, n_ep)]
+
+    def combine(c):
+        for j in range(local):
+            for copy in back[j, c]:
+                copy.wait_recv()
+        prod_s[:, col(c)] = dot(put, y_in[c].reshape(spots, CHUNK)).astype(jnp.bfloat16)
+
+    sum_over_tp(1, combine, lambda i, c: prod_s[block(i), col(c)].astype(jnp.float32), h_s.at[4], out_ref, gate_s)
+    back = sum(back.values(), [])
     for copy in sent + sum(there, []) + back:
         copy.wait_send()
     for spread in spreads:
@@ -379,21 +407,25 @@
     f32 = lambda *s: pltpu.VMEM(s, jnp.float32)
     dma = lambda *s: pltpu.SemaphoreType.DMA(s)
     shard = weights[-1].shape[1]
-    pieces = 2 * (n_tp - 1) + (n_ep // 2 - 1) * (n_tp - 1)
+    pieces = 3 * (n_tp - 1) + (n_ep // 2 - 1) * (n_tp - 1)
     spots = (n_ep, local, capacity, width)
+    chunks = width // CHUNK
+    split = (chunks, n_ep, local, capacity, CHUNK)
     return pl.pallas_call(
         functools.partial(block_kernel, n_tp, n_ep),
         out_shape=(OUT(h.shape, h.dtype), OUT(sk.shape, sk.dtype), OUT(sk.shape, sk.dtype)),
-        in_specs=[VMEM] * 7 + [ANY] * 16,
+        in_specs=[ANY] * 23,
         out_specs=(VMEM, VMEM, VMEM),
         scratch_shapes=[
             bf(*ck.shape), bf(*ck.shape), bf(2, 4, heads * dim, width), bf(4, n_tp, shard, width),
             *[bf(*w.shape) for w in dense], *[bf(*w.shape) for w in expert],
             f32(heads, dim, tokens), bf(heads, dim, tokens), bf(heads, dim, tokens), f32(heads, slots, tokens),
-            bf(4, n_tp, heads, dim, tokens), bf(2, n_tp, rows, width), bf(2, n_tp - 1, rows, width), bf(tokens, width), bf(5, tokens, width),
-            bf(*spots), bf(local, n_ep, capacity, width), bf(*spots), bf(*spots), f32(tokens, 1),
-            dma(18), dma(4, 2, heads), dma(4, n_tp - 1), dma(4, n_tp - 1), dma(4, heads, n_tp - 1), dma(4, heads, n_tp - 1),
-            dma(2 * local, n_ep - 1), dma(2 * local, n_ep - 1), dma(4, pieces), dma(4, pieces),
+            bf(4, n_tp, heads, dim, tokens), bf(2, chunks, n_tp, rows, CHUNK), bf(2, chunks, n_tp - 1, rows, CHUNK), bf(tokens, width), bf(5, tokens, width),
+            bf(*spots), bf(local, n_ep, capacity, width), bf(*split), bf(*split), f32(tokens, 1),
+            dma(25), dma(4, 2, heads), dma(4 * chunks, n_tp - 1), dma(4 * chunks, n_tp - 1),
+            dma(4, heads, tokens // LANES, n_tp - 1), dma(4, heads, tokens // LANES, n_tp - 1),
+            dma(local * (1 + chunks), n_ep - 1), dma(local * (1 + chunks), n_ep - 1), dma(4, pieces), dma(4, pieces),
+            *[pltpu.VMEM(a.shape, a.dtype) for a in (h, scale, pos, mask, bias, idx, router)],
         ],
         compiler_params=pltpu.CompilerParams(vmem_limit_bytes=VMEM_LIMIT, collective_id=0, has_side_effects=True),
         name="two_blocks",

time: 106 us -> 97 us (0.915)
  Pallas kernels: 99.2 us -> 90.1 us
    pallas_call x1, Pallas kernels: 99.2 us -> 90.1 us  [two_blocks(): pl.pallas_call(functools.partial(block_kernel, n_tp, n_ep), out_shape=(OU...]
where the time goes in v3:
time: 97 us; the launch traced here: 96.9 us
  Pallas kernels  90.1 us (93%)
  local copies, waits for them, and re-layouts  6.15 us (6%)
    pallas_call x1, Pallas kernels, two_blocks(): pl.pallas_call(functools.partial(block_kernel, n_tp, n_ep), out_shape=(OU...  90.1 us
    unnamed x3, local copies, waits for them, and re-layouts  6.15 us

profile of v3, /device:TPU:97, one launch (start us, length us, event | category | flops | bytes accessed | tf_op | source)
XLA Modules:
  0.0 96.9 jit_solution(2159129326358629143)
XLA Ops:
  0.6 90.1 %two_blocks.1 = (bf16[256,768]{1,0:T(8,128)(2,1)S(1)}, bf16[2,3,32,64,256]{4,3,2,1,0:T(8,128)(2,1)S(1)}, bf16[2,3,32,64,256]{4,3,2,1,0:T(8,128)(2,1)S(1)}) custom-call(bf16[256,768]{1,0:T(8,128)(2,1)} %refs_0_.1, f32[3,2,768]{2,1,0:T(2,128)} %bitcast.27, s32[1,256]{1,0:T(1,128)} %bitcast.28, s32[32,256]{1,0:T(8,128)} %bitcast.26, f32[3,32]{1,0:T(4,128)} %refs_4_.1, ...), custom_call_target="tpu_custom_call" | custom-call | tf_op jit(solution)/shard_map/two_blocks/pallas_call | solution.py:414
  90.8 0.7 copy.29
  91.5 2.7 %copy.30 = bf16[2,256,3,32,64]{1,4,3,2,0:T(8,128)(2,1)} copy(bf16[2,256,3,32,64]{1,4,3,2,0:T(8,128)(2,1)S(1)} %bitcast.16) | data formatting | bytes 12582912
  94.2 2.7 %copy.31 = bf16[2,256,3,32,64]{1,4,3,2,0:T(8,128)(2,1)} copy(bf16[2,256,3,32,64]{1,4,3,2,0:T(8,128)(2,1)S(1)} %bitcast.15) | data formatting | bytes 12582912

commit v4 on v3

--- a/solution.py
+++ b/solution.py
@@ -79,7 +79,7 @@
         self.rest = slice(rows, rows + direct)
         self.rows = pl.ds(pl.multiple_of(self.place * height, 16), height)
         self.cols = pl.ds(pl.multiple_of(self.half * width, LANES), width)
-        self.copies, self.used = [], 0
+        self.copies, self.used, self.extra = [], 0, []
 
     def _copy(self, src, dst, device):
         i = self.used
@@ -91,7 +91,9 @@
     def over_tp(self):
         tp = self.tp
         self.first = [self._copy(self.shard.at[self.rows, self.cols], self.full.at[tp.me, self.rows, self.cols], {tp.axis: tp.peer(k)}) for k in range(1, tp.n)]
-        self.extra = []
+
+    def over_tp_direct(self):
+        tp = self.tp
         if self.direct:
             self.extra = [self._copy(self.shard.at[self.rest, self.cols], self.full.at[tp.me, self.rest, self.cols], {tp.axis: tp.peer(k)}) for k in range(1, tp.n)]
 
@@ -141,7 +143,7 @@
     (wq_ref, wk_ref, wv_ref, wcq_ref, wo_ref, wco_ref, dg_ref, du_ref, dd_ref, eg_ref, eu_ref, ed_ref, sk_ref, sv_ref, ck_ref, cv_ref,
                  out_ref, ko_ref, vo_ref,
                  ck_buf, cv_buf, w_in, w_full, dg, du, dd, eg, eu, ed,
-                 q_s, k_s, v_s, b_s, ctx_s, part_s, in_s, prod_s, h_s, disp, x_in, y_out, y_in, gate_s,
+                 q_s, k_s, v_s, b_s, ctx_s, part_s, in_s, part_d, in_d, prod_s, h_s, disp, x_in, y_out, y_in, gate_s,
                  load_sem, cache_sem, tp_send, tp_recv, ctx_send, ctx_recv, ep_send, ep_recv, w_send, w_recv) = refs
     heads, slots, dim, tokens = sk_ref.shape[1:]
     width = h_ref.shape[1]
@@ -180,8 +182,9 @@
     load_caches(0, 0)
     pl.semaphore_wait(pltpu.get_barrier_semaphore(), n_tp + n_ep - 2)
 
-    spreads = [Spread(2 * layer + i, tp, ep, ref.at[layer], w_full.at[2 * layer + i], w_send, w_recv, 0 if layer + i else DIRECT) for layer in range(2) for i, ref in enumerate((wo_ref, wco_ref))]
+    spreads = [Spread(2 * layer + i, tp, ep, ref.at[layer], w_full.at[2 * layer + i], w_send, w_recv, 0 if layer else DIRECT) for layer in range(2) for i, ref in enumerate((wo_ref, wco_ref))]
     spreads[0].over_tp()
+    spreads[0].over_tp_direct()
     load(("full", 0), wo_ref.at[0], w_full.at[0, tp.me])
     load(("w", 0, 3), wcq_ref.at[0], w_in.at[0, 3])
 
@@ -193,11 +196,6 @@
         b_s[a] = dot(table, onehot, precision=lax.Precision.HIGHEST)
     slot_id = lax.broadcasted_iota(jnp.int32, (slots, LANES), 0)
 
-    def weighted(v_buf, a, cs, prob, acc):
-        for j in range(slots):
-            acc += v_buf[a, j, :, cs].astype(jnp.float32) * prob[j:j + 1, :]
-        return acc
-
     def context_copy(sub, a, b, k):
         mine = ctx_s.at[sub, tp.me, a, :, pl.ds(b * LANES, LANES)]
         return pltpu.make_async_remote_copy(src_ref=mine, dst_ref=mine, send_sem=ctx_send.at[sub, a, b, k - 1], recv_sem=ctx_recv.at[sub, a, b, k - 1], device_id={"tp": tp.peer(k)}, device_id_type=MESH)
@@ -206,79 +204,85 @@
         for k in range(1, n_tp):
             context_copy(sub, a, b, k).start()
 
-    def context_copies(sub):
-        return [context_copy(sub, a, b, k) for a in range(heads) for b in range(halves) for k in range(1, n_tp)]
-
-    def out_project(sub, h, out):
-        copies = context_copies(sub)
+    def lanes(b):
+        return slice(b * LANES, (b + 1) * LANES)
+
+    def out_project(sub, h, out, b):
+        copies = [context_copy(sub, a, b, k) for a in range(heads) for k in range(1, n_tp)]
         for copy in copies:
             copy.wait_recv()
-        spreads[sub].finish()
-        ready(("full", sub))
-        result = dot(ctx_s[sub].reshape(n_tp * heads * dim, tokens), w_full[sub].reshape(n_tp * heads * dim, width), TN)
-        out[...] = (h[...].astype(jnp.float32) + result.astype(jnp.bfloat16).astype(jnp.float32)).astype(jnp.bfloat16)
+        if b == 0:
+            spreads[sub].finish()
+            ready(("full", sub))
+        result = dot(ctx_s[sub, :, :, :, lanes(b)].reshape(n_tp * heads * dim, LANES), w_full[sub].reshape(n_tp * heads * dim, width), TN)
+        out[lanes(b), :] = (h[lanes(b), :].astype(jnp.float32) + result.astype(jnp.bfloat16).astype(jnp.float32)).astype(jnp.bfloat16)
         sent.extend(copies)
 
-    def self_attention(layer, h, between=None):
-        x = rms_norm(h[...], scale_ref[0, layer:layer + 1, :])
-        ready(*[("w", layer, i) for i in range(3)])
+    def self_attention(layer, h, b):
+        cs = lanes(b)
+        x = rms_norm(h[cs, :], scale_ref[0, layer:layer + 1, :])
+        if b == 0:
+            ready(*[("w", layer, i) for i in range(3)])
         qt, kt, vt = (dot(w_in[layer, i], x, NT).astype(jnp.bfloat16) for i in range(3))
         for a in range(heads):
-            q_s[a] = qt[a * dim:(a + 1) * dim, :].astype(jnp.float32)
-            k_s[a] = kt[a * dim:(a + 1) * dim, :]
-            v_s[a] = vt[a * dim:(a + 1) * dim, :]
+            q_s[a, :, cs] = qt[a * dim:(a + 1) * dim, :].astype(jnp.float32)
+            k_s[a, :, cs] = kt[a * dim:(a + 1) * dim, :]
+            v_s[a, :, cs] = vt[a * dim:(a + 1) * dim, :]
         kb, vb = ko_ref.at[layer], vo_ref.at[layer]
         sub = 2 * layer
+        pos = pos_ref[:, cs]
+        pos_bf = jnp.broadcast_to(pos.astype(jnp.float32), (dim, LANES)).astype(jnp.bfloat16)
 
         def one_head(a, carry):
-            cache_copies(0, layer, a).wait()
-            cache_copies(1, layer, a).wait()
-            for b in range(halves):
-                cs = slice(b * LANES, (b + 1) * LANES)
-                pos = pos_ref[:, cs]
-                pos_bf = jnp.broadcast_to(pos.astype(jnp.float32), (dim, LANES)).astype(jnp.bfloat16)
-                query, k_new, v_new = q_s[a, :, cs], k_s[a, :, cs], v_s[a, :, cs]
-                parts = []
-                for j in range(slots):
-                    old = kb[a, j, :, cs]
-                    kb[a, j, :, cs] = jnp.where(pos_bf == jnp.bfloat16(j), k_new, old)
-                    parts.append(jnp.sum(old.astype(jnp.float32) * query, axis=0, keepdims=True))
-                scores = jnp.concatenate(parts, axis=0)
-                at_slot = slot_id == pos
-                scores = jnp.where(at_slot, jnp.sum(k_new.astype(jnp.float32) * query, axis=0, keepdims=True), scores)
-                prob = softmax_rows(jnp.where(slot_id <= pos, scores + b_s[a, :, cs], NEG_BIG))
-                prob_new = jnp.sum(jnp.where(at_slot, prob, 0.0), axis=0, keepdims=True)
-                prob_old = jnp.where(at_slot, 0.0, prob)
-                acc = v_new.astype(jnp.float32) * prob_new
-                for j in range(slots):
-                    old = vb[a, j, :, cs]
-                    vb[a, j, :, cs] = jnp.where(pos_bf == jnp.bfloat16(j), v_new, old)
-                    acc += old.astype(jnp.float32) * prob_old[j:j + 1, :]
-                ctx_s[sub, tp.me, a, :, cs] = acc.astype(jnp.bfloat16)
-                send_context(sub, a, b)
+            if b == 0:
+                cache_copies(0, layer, a).wait()
+                cache_copies(1, layer, a).wait()
+            query, k_new, v_new = q_s[a, :, cs], k_s[a, :, cs], v_s[a, :, cs]
+            parts = []
+            for j in range(slots):
+                old = kb[a, j, :, cs]
+                kb[a, j, :, cs] = jnp.where(pos_bf == jnp.bfloat16(j), k_new, old)
+                parts.append(jnp.sum(old.astype(jnp.float32) * query, axis=0, keepdims=True))
+            scores = jnp.concatenate(parts, axis=0)
+            at_slot = slot_id == pos
+            scores = jnp.where(at_slot, jnp.sum(k_new.astype(jnp.float32) * query, axis=0, keepdims=True), scores)
+            prob = softmax_rows(jnp.where(slot_id <= pos, scores + b_s[a, :, cs], NEG_BIG))
+            prob_new = jnp.sum(jnp.where(at_slot, prob, 0.0), axis=0, keepdims=True)
+            prob_old = jnp.where(at_slot, 0.0, prob)
+            acc = v_new.astype(jnp.float32) * prob_new
+            for j in range(slots):
+                old = vb[a, j, :, cs]
+                vb[a, j, :, cs] = jnp.where(pos_bf == jnp.bfloat16(j), v_new, old)
+                acc += old.astype(jnp.float32) * prob_old[j:j + 1, :]
+            ctx_s[sub, tp.me, a, :, cs] = acc.astype(jnp.bfloat16)
+            send_context(sub, a, b)
             return carry
 
         lax.fori_loop(0, heads, one_head, 0)
 
-    def cross_attention(layer, h):
-        x = rms_norm(h[...], scale_ref[1, layer:layer + 1, :])
-        ready(("w", layer, 3))
+    def cross_attention(layer, h, b):
+        cs = lanes(b)
+        x = rms_norm(h[cs, :], scale_ref[1, layer:layer + 1, :])
+        if b == 0:
+            ready(("w", layer, 3))
         qt = dot(w_in[layer, 3], x, NT).astype(jnp.bfloat16)
         for a in range(heads):
-            q_s[a] = qt[a * dim:(a + 1) * dim, :].astype(jnp.float32)
+            q_s[a, :, cs] = qt[a * dim:(a + 1) * dim, :].astype(jnp.float32)
         kb, vb = ck_buf.at[layer], cv_buf.at[layer]
         sub = 2 * layer + 1
 
         def one_head(a, carry):
-            cache_copies(2, layer, a).wait()
-            cache_copies(3, layer, a).wait()
-            for b in range(halves):
-                cs = slice(b * LANES, (b + 1) * LANES)
-                query = q_s[a, :, cs]
-                scores = jnp.concatenate([jnp.sum(kb[a, j, :, cs].astype(jnp.float32) * query, axis=0, keepdims=True) for j in range(slots)], axis=0)
-                prob = softmax_rows(jnp.where(mask_ref[:, cs] > 0, scores, NEG_BIG))
-                ctx_s[sub, tp.me, a, :, cs] = weighted(vb, a, cs, prob, jnp.zeros((dim, LANES), jnp.float32)).astype(jnp.bfloat16)
-                send_context(sub, a, b)
+            if b == 0:
+                cache_copies(2, layer, a).wait()
+                cache_copies(3, layer, a).wait()
+            query = q_s[a, :, cs]
+            scores = jnp.concatenate([jnp.sum(kb[a, j, :, cs].astype(jnp.float32) * query, axis=0, keepdims=True) for j in range(slots)], axis=0)
+            prob = softmax_rows(jnp.where(mask_ref[:, cs] > 0, scores, NEG_BIG))
+            acc = jnp.zeros((dim, LANES), jnp.float32)
+            for j in range(slots):
+                acc += vb[a, j, :, cs].astype(jnp.float32) * prob[j:j + 1, :]
+            ctx_s[sub, tp.me, a, :, cs] = acc.astype(jnp.bfloat16)
+            send_context(sub, a, b)
             return carry
 
         lax.fori_loop(0, heads, one_head, 0)
@@ -289,35 +293,60 @@
     chunks = width // CHUNK
     order = [n_tp // 2] + [k for k in range(1, n_tp) if k != n_tp // 2]
 
-    def sum_over_tp(phase, prepare, part, h, out, gate=None, between=lambda: None):
+    def sum_over_tp(prepare, part, h, out, gate):
         gathers, spreads_out = [], []
         for c in range(chunks):
             prepare(c)
             for k in order:
-                part_s[phase, c, k] = part(tp.peer(k), c).astype(jnp.bfloat16)
-                gathers.append(tp.copy_to((2 * phase) * chunks + c, k, part_s.at[phase, c, k], in_s.at[phase, c, k - 1]))
+                part_s[c, k] = part(tp.peer(k), c).astype(jnp.bfloat16)
+                gathers.append(tp.copy_to(2 * halves + c, k, part_s.at[c, k], in_s.at[c, k - 1]))
         own = [part(tp.me, c) for c in range(chunks)]
-        between()
         for c in range(chunks):
             for copy in gathers[c * (n_tp - 1):(c + 1) * (n_tp - 1)]:
                 copy.wait_recv()
             total = own[c]
             for k in range(n_tp - 1):
-                total += in_s[phase, c, k].astype(jnp.float32)
+                total += in_s[c, k].astype(jnp.float32)
             total = total.astype(jnp.bfloat16).astype(jnp.float32)
-            if gate is not None:
-                total = total * gate[block(tp.me), :]
+            total = total * gate[block(tp.me), :]
             out[block(tp.me), col(c)] = (h[block(tp.me), col(c)].astype(jnp.float32) + total).astype(jnp.bfloat16)
             mine = out.at[block(tp.me), col(c)]
-            spreads_out += [tp.copy_to((2 * phase + 1) * chunks + c, k, mine, mine) for k in order]
+            spreads_out += [tp.copy_to(2 * halves + chunks + c, k, mine, mine) for k in order]
         for copy in spreads_out:
             copy.wait_recv()
         sent.extend(gathers + spreads_out)
 
-    self_attention(0, h_ref)
+    own_rows = rows // halves
+    half_block = lambda b, i: pl.ds(pl.multiple_of(b * LANES + i * own_rows, own_rows), own_rows)
+    half_in, half_out = {}, {}
+
+    def half_parts(b, part):
+        part_d[b] = part.astype(jnp.bfloat16)
+        there = lambda k: part_d.at[b, pl.ds(pl.multiple_of(tp.peer(k) * own_rows, own_rows), own_rows)]
+        half_in[b] = [tp.copy_to(b, k, there(k), in_d.at[b, k - 1]) for k in order]
+
+    def half_sums(b, h, out):
+        for copy in half_in[b]:
+            copy.wait_recv()
+        total = part_d[b, pl.ds(pl.multiple_of(tp.me * own_rows, own_rows), own_rows), :].astype(jnp.float32)
+        for k in range(n_tp - 1):
+            total += in_d[b, k].astype(jnp.float32)
+        mine = half_block(b, tp.me)
+        out[mine, :] = (h[mine, :].astype(jnp.float32) + total.astype(jnp.bfloat16).astype(jnp.float32)).astype(jnp.bfloat16)
+        half_out[b] = [tp.copy_to(halves + b, k, out.at[mine], out.at[mine]) for k in order]
+
+    def half_arrived(b):
+        for copy in half_out[b]:
+            copy.wait_recv()
+        sent.extend(half_in[b] + half_out[b])
+
+    self_attention(0, h_ref, 0)
+    spreads[1].over_tp()
+    for b in range(1, halves):
+        self_attention(0, h_ref, b)
     spreads[0].along_ep()
-    for n in (1, 2, 3):
-        spreads[n].over_tp()
+    spreads[2].over_tp()
+    spreads[1].over_tp_direct()
     load(("full", 1), wco_ref.at[0], w_full.at[1, tp.me])
     load_caches(2, 0)
     for name, ref, dst in (("dg", dg_ref, dg), ("du", du_ref, du), ("dd", dd_ref, dd)):
@@ -326,36 +355,43 @@
         load(("w", 1, i), ref.at[1], w_in.at[1, i])
     spreads[0].to_neighbour()
     spreads[1].along_ep()
-    out_project(0, h_ref, h_s.at[0])
+    for b in range(halves):
+        out_project(0, h_ref, h_s.at[0], b)
+        cross_attention(0, h_s.at[0], b)
     load(("full", 2), wo_ref.at[1], w_full.at[2, tp.me])
     load(("full", 3), wco_ref.at[1], w_full.at[3, tp.me])
     load_caches(0, 1)
-    cross_attention(0, h_s.at[0])
     spreads[1].to_neighbour()
     spreads[2].along_ep()
-    out_project(1, h_s.at[0], h_s.at[1])
     load_caches(2, 1)
     for name, ref, dst in (("eg", eg_ref, eg), ("eu", eu_ref, eu), ("ed", ed_ref, ed)):
         load(name, ref, dst)
-    x = rms_norm(h_s[1], scale_ref[2, 0:1, :])
-    ready("dg", "du", "dd")
-    prod_s[...] = gelu_product(dot(x, dg[...]), dot(x, du[...]))
-
-    def move_weights():
-        spreads[2].to_neighbour()
-        spreads[3].along_ep()
-
-    sum_over_tp(0, lambda c: None, lambda i, c: dot(prod_s[block(i), :], dd[:, col(c)]), h_s.at[1], h_s.at[2], between=move_weights)
-
-    self_attention(1, h_s.at[2])
+    for b in range(halves):
+        out_project(1, h_s.at[0], h_s.at[1], b)
+        x = rms_norm(h_s[1, lanes(b), :], scale_ref[2, 0:1, :])
+        if b == 0:
+            ready("dg", "du", "dd")
+        half_parts(b, dot(gelu_product(dot(x, dg[...]), dot(x, du[...])), dd[...]))
+        if b == 0:
+            spreads[3].over_tp()
+    for b in range(halves):
+        half_sums(b, h_s.at[1], h_s.at[2])
+        if b == 0:
+            spreads[3].along_ep()
+            spreads[2].to_neighbour()
+    for b in range(halves):
+        half_arrived(b)
+        self_attention(1, h_s.at[2], b)
     spreads[3].to_neighbour()
-    out_project(2, h_s.at[2], h_s.at[3])
-    cross_attention(1, h_s.at[3])
+    for b in range(halves):
+        out_project(2, h_s.at[2], h_s.at[3], b)
+        cross_attention(1, h_s.at[3], b)
     experts = router_ref.shape[0]
     local = experts // n_ep
     place, one_t, capacity = routing(idx_ref[...], experts)
     spots = experts * capacity
-    out_project(3, h_s.at[3], h_s.at[4])
+    for b in range(halves):
+        out_project(3, h_s.at[3], h_s.at[4], b)
     x = rms_norm(h_s[4], scale_ref[2, 1:2, :])
     pick = to_bf(lax.broadcasted_iota(jnp.int32, (spots, tokens), 0).astype(jnp.float32) == place)
     disp[...] = dot(pick, x).astype(jnp.bfloat16).reshape(disp.shape)
@@ -386,7 +422,7 @@
                 copy.wait_recv()
         prod_s[:, col(c)] = dot(put, y_in[c].reshape(spots, CHUNK)).astype(jnp.bfloat16)
 
-    sum_over_tp(1, combine, lambda i, c: prod_s[block(i), col(c)].astype(jnp.float32), h_s.at[4], out_ref, gate_s)
+    sum_over_tp(combine, lambda i, c: prod_s[block(i), col(c)].astype(jnp.float32), h_s.at[4], out_ref, gate_s)
     back = sum(back.values(), [])
     for copy in sent + sum(there, []) + back:
         copy.wait_send()
@@ -409,7 +445,7 @@
     shard = weights[-1].shape[1]
     pieces = 3 * (n_tp - 1) + (n_ep // 2 - 1) * (n_tp - 1)
     spots = (n_ep, local, capacity, width)
-    chunks = width // CHUNK
+    chunks, halves = width // CHUNK, tokens // LANES
     split = (chunks, n_ep, local, capacity, CHUNK)
     return pl.pallas_call(
         functools.partial(block_kernel, n_tp, n_ep),
@@ -420,9 +456,9 @@
             bf(*ck.shape), bf(*ck.shape), bf(2, 4, heads * dim, width), bf(4, n_tp, shard, width),
             *[bf(*w.shape) for w in dense], *[bf(*w.shape) for w in expert],
             f32(heads, dim, tokens), bf(heads, dim, tokens), bf(heads, dim, tokens), f32(heads, slots, tokens),
-            bf(4, n_tp, heads, dim, tokens), bf(2, chunks, n_tp, rows, CHUNK), bf(2, chunks, n_tp - 1, rows, CHUNK), bf(tokens, width), bf(5, tokens, width),
+            bf(4, n_tp, heads, dim, tokens), bf(chunks, n_tp, rows, CHUNK), bf(chunks, n_tp - 1, rows, CHUNK), bf(halves, LANES, width), bf(halves, n_tp - 1, LANES // n_tp, width), bf(tokens, width), bf(5, tokens, width),
             bf(*spots), bf(local, n_ep, capacity, width), bf(*split), bf(*split), f32(tokens, 1),
-            dma(25), dma(4, 2, heads), dma(4 * chunks, n_tp - 1), dma(4 * chunks, n_tp - 1),
+            dma(25), dma(4, 2, heads), dma(2 * (halves + chunks), n_tp - 1), dma(2 * (halves + chunks), n_tp - 1),
             dma(4, heads, tokens // LANES, n_tp - 1), dma(4, heads, tokens // LANES, n_tp - 1),
             dma(local * (1 + chunks), n_ep - 1), dma(local * (1 + chunks), n_ep - 1), dma(4, pieces), dma(4, pieces),
             *[pltpu.VMEM(a.shape, a.dtype) for a in (h, scale, pos, mask, bias, idx, router)],

time: 97 us -> 91.2 us (0.940)
  Pallas kernels: 90.1 us -> 84.3 us
    pallas_call x1, Pallas kernels: 90.1 us -> 84.3 us  [two_blocks(): pl.pallas_call(functools.partial(block_kernel, n_tp, n_ep), out_shape=(OU...]
where the time goes in v4:
time: 91.2 us; the launch traced here: 91.1 us
  Pallas kernels  84.3 us (92%)
  local copies, waits for them, and re-layouts  6.15 us (7%)
    pallas_call x1, Pallas kernels, two_blocks(): pl.pallas_call(functools.partial(block_kernel, n_tp, n_ep), out_shape=(OU...  84.3 us
    unnamed x3, local copies, waits for them, and re-layouts  6.15 us

profile of v4, /device:TPU:97, one launch (start us, length us, event | category | flops | bytes accessed | tf_op | source)
XLA Modules:
  0.0 91.1 jit_solution(9739178802075314721)
XLA Ops:
  0.6 84.3 %two_blocks.1 = (bf16[256,768]{1,0:T(8,128)(2,1)S(1)}, bf16[2,3,32,64,256]{4,3,2,1,0:T(8,128)(2,1)S(1)}, bf16[2,3,32,64,256]{4,3,2,1,0:T(8,128)(2,1)S(1)}) custom-call(bf16[256,768]{1,0:T(8,128)(2,1)} %refs_0_.1, f32[3,2,768]{2,1,0:T(2,128)} %bitcast.27, s32[1,256]{1,0:T(1,128)} %bitcast.28, s32[32,256]{1,0:T(8,128)} %bitcast.26, f32[3,32]{1,0:T(4,128)} %refs_4_.1, ...), custom_call_target="tpu_custom_call" | custom-call | tf_op jit(solution)/shard_map/two_blocks/pallas_call | solution.py:450
  84.9 0.7 copy.29
  85.7 2.7 %copy.30 = bf16[2,256,3,32,64]{1,4,3,2,0:T(8,128)(2,1)} copy(bf16[2,256,3,32,64]{1,4,3,2,0:T(8,128)(2,1)S(1)} %bitcast.16) | data formatting | bytes 12582912
  88.4 2.7 %copy.31 = bf16[2,256,3,32,64]{1,4,3,2,0:T(8,128)(2,1)} copy(bf16[2,256,3,32,64]{1,4,3,2,0:T(8,128)(2,1)S(1)} %bitcast.15) | data formatting | bytes 12582912
